TPU v7x, 512 devices: a whole 4x8x8 slice. The times are simulated.
512 devices in a mesh: gx: 16 (over y_lo, z), gy: 4 (over x), col: 8 (over y_hi, core).
Axes of the slice: x: 4, y: 8 (y_hi: 4, y_lo: 2; y = y_hi * 2 + y_lo), z: 8, core: 2. Of those that a mesh axis runs over, the one named last changes fastest.
Arguments:
- fields: bfloat16 [8, 128, 128, 32, 128], P('col', 'gx', 'gy'), may hold values from -6 to 6
- spectral: bfloat16 [1, 16, 16, 2, 32, 32, 16], P(None, 'gx', 'gy', None, None, 'col'), may hold values from -0.75 to 0.75
- skip_weight: bfloat16 [1, 32, 32], replicated, may hold values from -1 to 1
- skip_bias: float32 [1, 32], replicated, may hold values from -3 to 3
- norm_gain: float32 [1, 32], replicated, may hold values from 0.5 to 1.5
- norm_shift: float32 [1, 32], replicated, may hold values from -3 to 3
Outputs:
- activations: bfloat16 [8, 128, 128, 32, 128], P('col', 'gx', 'gy')
All inputs are finite; a program needn't handle non-finite values.
Results may differ from a plain program's by a relative error of at most 0.012.
Values may be sent and summed in bfloat16 or wider, within the bound.
No kernel may reach another device: no remote copies, remote signals or barrier semaphores. Data moves between devices by JAX's collectives and lax.ppermute only.
A program may use at most 64 MiB of HBM per device.

v0:
```python
import math

import jax
import jax.numpy as jnp
from jax import lax
from jax.sharding import PartitionSpec as P

X = 128
Y = 128
Z = 128
MX = 16
MY = 16
MZ = 16


norm_eps = 1e-05


def cut_along(shard, dim, length):
    before, after = (shard.shape[:dim], shard.shape[dim + 1 :])
    return jnp.moveaxis(shard.reshape(*before, length, -1, *after), dim, 0)


def summed_on_arrival(shard, axis, dim):
    length = lax.axis_size(axis)
    parts = lax.all_to_all(cut_along(shard, dim, length), axis, 0, 0, tiled=True)
    return jnp.sum(parts.astype(jnp.float32), axis=0)


def copy_for_each(shard, axis):
    copies = jnp.broadcast_to(shard, (lax.axis_size(axis), *shard.shape))
    return lax.all_to_all(copies, axis, split_axis=0, concat_axis=0, tiled=True)


def joined_along(parts, dim):
    shape = list(parts.shape[1:])
    shape[dim] *= parts.shape[0]
    return jnp.moveaxis(parts, 0, dim).reshape(shape)


def collect(shard, axis, dim):
    parts = copy_for_each(shard, axis)
    return joined_along(parts, dim)


def signed_freqs(count):
    index = jnp.arange(count, dtype=jnp.int32)
    return jnp.where(index < count // 2, index, index - count)


def angles(positions, frequency, length):
    turn_count = positions[:, None] * frequency[None, :] % length
    return turn_count.astype(jnp.float32) * (2.0 * math.pi / length)


def forward_table(positions, frequency, length, factor):
    phase_angle = angles(positions, frequency, length)
    cosine = jnp.cos(phase_angle) * factor
    sine_part = jnp.sin(phase_angle) * factor
    from_real = jnp.stack([cosine, -sine_part], axis=-1)
    from_imag = jnp.stack([sine_part, cosine], axis=-1)
    return jnp.stack([from_real, from_imag], axis=1)


def inverse_table(frequency, positions, length):
    phase_angle = angles(positions, frequency, length).T
    cosine = jnp.cos(phase_angle)
    sine_part = jnp.sin(phase_angle)
    from_real = jnp.stack([cosine, sine_part], axis=-1)
    from_imag = jnp.stack([-sine_part, cosine], axis=-1)
    return jnp.stack([from_real, from_imag], axis=1)


def depth_tables(length, count):
    frequency = jnp.arange(count, dtype=jnp.int32)
    phase_angle = angles(jnp.arange(length, dtype=jnp.int32), frequency, length)
    forward = jnp.concatenate([jnp.cos(phase_angle), -jnp.sin(phase_angle)], axis=1)
    backward = jnp.concatenate([jnp.cos(phase_angle).T, -jnp.sin(phase_angle).T], axis=0)
    return (forward.astype(jnp.bfloat16), backward.astype(jnp.bfloat16))


def mix_modes(spectrum, weight):

    def contract(left, right):
        return jnp.einsum("abcz,abcdz->abdz", left, right, preferred_element_type=jnp.float32)

    real_in = spectrum[:, :, :, 0]
    imag_in = spectrum[:, :, :, 1]
    real_weight = weight[:, :, 0]
    imag_weight = weight[:, :, 1]
    real_out = contract(real_in, real_weight) - contract(imag_in, imag_weight)
    imag_out = contract(real_in, imag_weight) + contract(imag_in, real_weight)
    return jnp.stack([real_out, imag_out], axis=3)


def finish(spectral_part, skip_part, offset, scaling, shift_term):
    pre_norm = spectral_part + skip_part + offset[:, None]
    centre = jnp.mean(pre_norm, axis=2, keepdims=True)
    spread = jnp.mean(jnp.square(pre_norm - centre), axis=2, keepdims=True)
    normed = (pre_norm - centre) * lax.rsqrt(spread + norm_eps) * scaling[:, None] + shift_term[
        :, None
    ]
    return jax.nn.gelu(normed, approximate=False).astype(jnp.bfloat16)


def local(fields, spectral, skip_weight, skip_bias, norm_gain, norm_shift):
    hidden = fields[0]
    tile_first, tile_second, channels, depth_cells = hidden.shape
    first_cells = lax.axis_index("gx") * tile_first + jnp.arange(tile_first, dtype=jnp.int32)
    second_cells = lax.axis_index("gy") * tile_second + jnp.arange(tile_second, dtype=jnp.int32)
    depth_forward, depth_backward = depth_tables(Z, MZ)
    second_forward = forward_table(second_cells, signed_freqs(MY), Y, 1.0).astype(jnp.bfloat16)
    first_forward = forward_table(first_cells, signed_freqs(MX), X, 1.0 / math.sqrt(X * Y * Z))
    first_inverse = inverse_table(signed_freqs(MX), first_cells, X).astype(jnp.bfloat16)
    second_inverse = inverse_table(signed_freqs(MY), second_cells, Y)
    inverse_scale = 1.0 / math.sqrt(MX * MY * MZ)
    amplitude = jnp.dot(
        hidden.reshape(-1, depth_cells), depth_forward, preferred_element_type=jnp.float32
    )
    amplitude = amplitude.astype(jnp.bfloat16).reshape(tile_first, tile_second, channels, 2, MZ)
    along_second = jnp.einsum(
        "xycrz,yrks->xkcsz", amplitude, second_forward, preferred_element_type=jnp.float32
    )
    summed_second = summed_on_arrival(along_second.astype(jnp.bfloat16), "gy", 1)
    partial_modes = jnp.einsum("xkcsz,xsjt->jkctz", summed_second, first_forward)
    summed = summed_on_arrival(partial_modes.astype(jnp.bfloat16), "gx", 0)
    spectrum = summed.astype(jnp.bfloat16)
    weights_here = spectral[0]
    mixed_modes = mix_modes(spectrum, collect(weights_here, "col", 4)).astype(jnp.bfloat16)
    gathered_second = collect(mixed_modes, "gy", 1)
    full_modes = collect(gathered_second, "gx", 0)
    rows_first = jnp.einsum(
        "jkcsz,jsxt->xkctz", full_modes, first_inverse, preferred_element_type=jnp.float32
    )
    rows_both = jnp.einsum("xkcsz,ksyt->xyctz", rows_first, second_inverse).astype(jnp.bfloat16)
    spectral_part = jnp.dot(
        rows_both.reshape(-1, 2 * MZ), depth_backward, preferred_element_type=jnp.float32
    )
    spectral_part = (
        spectral_part.reshape(tile_first, tile_second, channels, depth_cells) * inverse_scale
    )
    skip_part = jnp.einsum(
        "oc,xycz->xyoz", skip_weight[0], hidden, preferred_element_type=jnp.float32
    )
    hidden = finish(spectral_part, skip_part, skip_bias[0], norm_gain[0], norm_shift[0])
    return hidden[None]


def solution(mesh):
    placed = (
        P("col", "gx", "gy", None, None),
        P(None, "gx", "gy", None, None, "col", None),
        P(),
        P(),
        P(),
        P(),
    )
    return jax.shard_map(
        local,
        mesh=mesh,
        in_specs=placed,
        out_specs=P("col", "gx", "gy", None, None),
        check_vma=False,
    )
```

profile of v0, /device:TPU:24, one launch (start us, length us, event | category | flops | bytes accessed | tf_op | source)
XLA Modules:
  0.0 119.3 jit_solution(9642873758831152271)
XLA Ops:
  0.1 1.5 %copy-done = bf16[1,8,32,32,128]{4,3,2,1,0:T(8,128)(2,1)S(1)} copy-done((bf16[1,8,32,32,128]{4,3,2,1,0:T(8,128)(2,1)S(1)}, bf16[1,8,32,32,128]{4,3,2,1,0:T(8,128)(2,1)}, u32[]{:S(2)}) %copy-start) | copy-done | bytes 2097176
  2.4 2.6 %reshape.787 = bf16[8,32,32,2,16]{2,1,0,4,3:T(8,128)(2,1)} reshape(bf16[8192,32]{0,1:T(8,128)(2,1)S(1)} %fusion) | data formatting | bytes 1048576 | tf_op jit(solution)/shard_map/reshape | solution.py:120
  5.2 2.1 %bitcast_convert_fusion.1 = bf16[16,2,8,32,16]{3,0,4,2,1:T(8,128)(2,1)S(1)} fusion(bf16[8,32,32,2,16]{2,1,0,4,3:T(8,128)(2,1)} %reshape.787, bf16[32,1,16,2]{0,2,1,3:T(8,128)(2,1)S(1)} %get-tuple-element.12, bf16[32,1,16,2]{0,2,1,3:T(8,128)(2,1)S(1)} %get-tuple-element.11), kind=kOutput, calls=%fused_computation.30 | convolution fusion | flops 16916480 | bytes 790528 | tf_op jit(solution)/shard_map/xycrz,yrks->xkcsz/dot_general | solution.py:121
  7.8 1.7 %reshape.818 = bf16[4,2,16384]{2,1,0:T(2,128)(2,1)} reshape(bf16[4,2,8,16,4,32]{5,4,3,2,1,0:T(4,128)(2,1)S(1)} %bitcast.195) | data formatting | bytes 524288
  9.5 4.3 %all-to-all-start = ((bf16[4,2,16384]{2,1,0:T(2,128)(2,1)}), bf16[4,2,16384]{2,1,0:T(2,128)(2,1)S(1)}, u32[]{:S(2)}, u32[]{:S(2)}) async-start(bf16[4,2,16384]{2,1,0:T(2,128)(2,1)} %reshape.818), calls=%async_computation | async-start | bytes 524288 | tf_op jit(solution)/shard_map/all_to_all | solution.py:26
  13.9 6.5 %all-to-all-done = bf16[4,2,16384]{2,1,0:T(2,128)(2,1)S(1)} async-done(((bf16[4,2,16384]{2,1,0:T(2,128)(2,1)}), bf16[4,2,16384]{2,1,0:T(2,128)(2,1)S(1)}, u32[]{:S(2)}, u32[]{:S(2)}) %all-to-all-start) | async-done | bytes 262176 | tf_op jit(solution)/shard_map/all_to_all | solution.py:26
  22.9 11.8 %all-to-all-start.1 = ((bf16[16,2,2048]{2,1,0:T(2,128)(2,1)}), bf16[16,2,2048]{2,1,0:T(2,128)(2,1)S(1)}, u32[]{:S(2)}, u32[]{:S(2)}) async-start(bf16[16,2,2048]{2,1,0:T(2,128)(2,1)} %reshape.820), calls=%async_computation.1 | async-start | bytes 262144 | tf_op jit(solution)/shard_map/all_to_all | solution.py:26
  35.8 1.7 %reshape.816 = bf16[8,2,8192]{2,1,0:T(2,128)(2,1)} reshape(bf16[8,1,4,2,4,16,32]{6,5,4,3,2,1,0:T(8,128)(2,1)S(1)} %broadcast_bitcast_fusion.1) | data formatting | bytes 524288
  37.5 4.8 %all-to-all-done.1 = bf16[16,2,2048]{2,1,0:T(2,128)(2,1)S(1)} async-done(((bf16[16,2,2048]{2,1,0:T(2,128)(2,1)}), bf16[16,2,2048]{2,1,0:T(2,128)(2,1)S(1)}, u32[]{:S(2)}, u32[]{:S(2)}) %all-to-all-start.1) | async-done | bytes 131104 | tf_op jit(solution)/shard_map/all_to_all | solution.py:26
  42.2 6.5 %all-to-all-start.2 = ((bf16[8,2,8192]{2,1,0:T(2,128)(2,1)}), bf16[8,2,8192]{2,1,0:T(2,128)(2,1)S(1)}, u32[]{:S(2)}, u32[]{:S(2)}) async-start(bf16[8,2,8192]{2,1,0:T(2,128)(2,1)} %reshape.816), calls=%async_computation.2 | async-start | bytes 524288 | tf_op jit(solution)/shard_map/all_to_all | solution.py:32
  49.2 9.5 %all-to-all-done.2 = bf16[8,2,8192]{2,1,0:T(2,128)(2,1)S(1)} async-done(((bf16[8,2,8192]{2,1,0:T(2,128)(2,1)}), bf16[8,2,8192]{2,1,0:T(2,128)(2,1)S(1)}, u32[]{:S(2)}, u32[]{:S(2)}) %all-to-all-start.2) | async-done | bytes 262176 | tf_op jit(solution)/shard_map/all_to_all | solution.py:32
  59.6 1.2 %copy.56 = bf16[4,32,32,16]{2,1,3,0:T(8,128)(2,1)} copy(bf16[4,32,32,16]{1,3,2,0:T(8,128)(2,1)S(1)} %get-tuple-element.5) | data formatting | bytes 262144 | tf_op jit(solution)/shard_map/reshape.1
  61.3 1.3 %fusion.34 = f32[4,16,1,32]{3,2,1,0:T(1,128)S(1)} fusion(bf16[4,32,32,16]{2,1,3,0:T(8,128)(2,1)} %copy.56, bf16[4,32,16,1]{1,2,0,3:T(8,128)(2,1)S(1)} %get-tuple-element.7), kind=kOutput, calls=%fused_computation.55 | convolution fusion | flops 131072 | bytes 143360 | tf_op jit(solution)/shard_map/abcz,abcdz->abdz/dot_general | solution.py:85
  62.6 1.3 %fusion.40 = f32[4,16,1,32]{3,2,1,0:T(1,128)S(1)} fusion(bf16[4,32,32,16]{2,1,3,0:T(8,128)(2,1)} %copy.56, bf16[4,32,16,1]{1,2,0,3:T(8,128)(2,1)S(1)} %get-tuple-element.8), kind=kOutput, calls=%fused_computation.61 | convolution fusion | flops 131072 | bytes 143360 | tf_op jit(solution)/shard_map/abcz,abcdz->abdz/dot_general | solution.py:85
  64.6 7.8 %all_to_all.25 = bf16[4,2,2048]{2,1,0:T(2,128)(2,1)S(1)} all-to-all(bf16[4,2,2048]{2,1,0:T(2,128)(2,1)S(1)} %reshape.822), channel_id=1, replica_groups=mesh['gx'=16,'gy'=4,'col'=8] {'gy'}, dimensions={0} | all-to-all | bytes 65536 | tf_op jit(solution)/shard_map/all_to_all | solution.py:32
  72.6 1.7 %broadcast_bitcast_fusion = bf16[16,1,16,2,16,32]{5,4,3,2,1,0:T(8,128)(2,1)} fusion(bf16[16,32,2,16]{1,3,2,0:T(8,128)(2,1)S(1)} %bitcast.199), kind=kLoop, calls=%fused_computation.169 | loop fusion | bytes 557056
  74.3 4.5 %reshape.824 = bf16[16,2,8192]{2,1,0:T(2,128)(2,1)} reshape(bf16[16,1,16,2,16,32]{5,4,3,2,1,0:T(8,128)(2,1)} %broadcast_bitcast_fusion) | data formatting | bytes 1048576
  78.8 5.0 %all-to-all-start.4 = ((bf16[16,2,8192]{2,1,0:T(2,128)(2,1)}), bf16[16,2,8192]{2,1,0:T(2,128)(2,1)S(1)}, u32[]{:S(2)}, u32[]{:S(2)}) async-start(bf16[16,2,8192]{2,1,0:T(2,128)(2,1)} %reshape.824), calls=%async_computation.4 | async-start | bytes 1048576 | tf_op jit(solution)/shard_map/all_to_all | solution.py:32
  84.1 13.9 %all-to-all-done.4 = bf16[16,2,8192]{2,1,0:T(2,128)(2,1)S(1)} async-done(((bf16[16,2,8192]{2,1,0:T(2,128)(2,1)}), bf16[16,2,8192]{2,1,0:T(2,128)(2,1)S(1)}, u32[]{:S(2)}, u32[]{:S(2)}) %all-to-all-start.4) | async-done | bytes 524320 | tf_op jit(solution)/shard_map/all_to_all | solution.py:32
  98.0 2.0 %reshape.825 = bf16[16,1,16,2,16,32]{5,4,3,2,1,0:T(8,128)(2,1)} reshape(bf16[16,2,8192]{2,1,0:T(2,128)(2,1)S(1)} %all-to-all-done.4) | data formatting | bytes 1048576
  100.0 2.9 %fusion.22 = bf16[8,16,32,2,16]{2,0,4,1,3:T(8,128)(2,1)S(1)} fusion(bf16[16,1,16,32,2,16]{3,5,4,2,1,0:T(8,128)(2,1)} %bitcast.191, bf16[16,1,8,2]{0,2,3,1:T(8,128)(2,1)S(1)} %get-tuple-element.14, bf16[16,1,8,2]{0,2,3,1:T(8,128)(2,1)S(1)} %get-tuple-element.13), kind=kOutput, calls=%fused_computation.38 | convolution fusion | flops 8389120 | bytes 787456 | tf_op jit(solution)/shard_map/jkcsz,jsxt->xkctz/dot_general | solution.py:132
  102.9 1.8 %fusion.25 = bf16[8,32,32,2,16]{2,1,4,0,3:T(8,128)(2,1)S(1)} fusion(bf16[8,16,32,2,16]{2,0,4,1,3:T(8,128)(2,1)S(1)} %fusion.22, bf16[16,1,32,2]{2,0,1,3:T(8,128)(2,1)S(1)} %get-tuple-element.10, bf16[16,1,32,2]{2,0,1,3:T(8,128)(2,1)S(1)} %get-tuple-element.9), kind=kOutput, calls=%fused_computation.39 | convolution fusion | flops 16785408 | bytes 790528 | tf_op jit(solution)/shard_map/xkcsz,ksyt->xyctz/dot_general | solution.py:135
  107.4 1.2 %multiply_reduce_fusion = f32[8,32,128]{2,1,0:T(8,128)S(1)} fusion(f32[8,32,32,128]{3,2,1,0:T(8,128)S(1)} %get-tuple-element.30, f32[8,32,128]{2,1,0:T(8,128)S(1)} %broadcast_multiply_fusion), kind=kLoop, calls=%fused_computation.23 | loop fusion | flops 3112960 | bytes 4456448 | tf_op jit(solution)/shard_map/reduce_sum | solution.py:99
  108.7 10.6 %fusion.21 = bf16[1,8,32,32,128]{4,3,2,1,0:T(8,128)(2,1)} fusion(f32[32]{0:T(128)S(1)} %bitcast.207, f32[32]{0:T(128)S(1)} %bitcast.208, f32[8,32,128]{2,1,0:T(8,128)S(1)} %add_rsqrt_fusion, f32[8,32,32,128]{3,2,1,0:T(8,128)S(1)} %get-tuple-element.30, f32[8,32,128]{2,1,0:T(8,128)S(1)} %broadcast_multiply_fusion), kind=kLoop, calls=%fused_computation.37 | loop fusion | flops 72351744 | bytes 6553856 | tf_op jit(solution)/shard_map/broadcast_in_dim | solution.py:146
  (50 shorter events, 10.9 us)
Async XLA Ops:
  0.0 1.6 %copy-start = (bf16[1,8,32,32,128]{4,3,2,1,0:T(8,128)(2,1)S(1)}, bf16[1,8,32,32,128]{4,3,2,1,0:T(8,128)(2,1)}, u32[]{:S(2)}) copy-start(bf16[1,8,32,32,128]{4,3,2,1,0:T(8,128)(2,1)} %param.6) | copy-start | bytes 6291460
  9.5 11.0 %all-to-all-start = ((bf16[4,2,16384]{2,1,0:T(2,128)(2,1)}), bf16[4,2,16384]{2,1,0:T(2,128)(2,1)S(1)}, u32[]{:S(2)}, u32[]{:S(2)}) async-start(bf16[4,2,16384]{2,1,0:T(2,128)(2,1)} %reshape.818), calls=%async_computation | async-start | bytes 524288 | tf_op jit(solution)/shard_map/all_to_all | solution.py:26
  22.9 19.4 %all-to-all-start.1 = ((bf16[16,2,2048]{2,1,0:T(2,128)(2,1)}), bf16[16,2,2048]{2,1,0:T(2,128)(2,1)S(1)}, u32[]{:S(2)}, u32[]{:S(2)}) async-start(bf16[16,2,2048]{2,1,0:T(2,128)(2,1)} %reshape.820), calls=%async_computation.1 | async-start | bytes 262144 | tf_op jit(solution)/shard_map/all_to_all | solution.py:26
  42.2 16.4 %all-to-all-start.2 = ((bf16[8,2,8192]{2,1,0:T(2,128)(2,1)}), bf16[8,2,8192]{2,1,0:T(2,128)(2,1)S(1)}, u32[]{:S(2)}, u32[]{:S(2)}) async-start(bf16[8,2,8192]{2,1,0:T(2,128)(2,1)} %reshape.816), calls=%async_computation.2 | async-start | bytes 524288 | tf_op jit(solution)/shard_map/all_to_all | solution.py:32
  78.8 19.2 %all-to-all-start.4 = ((bf16[16,2,8192]{2,1,0:T(2,128)(2,1)}), bf16[16,2,8192]{2,1,0:T(2,128)(2,1)S(1)}, u32[]{:S(2)}, u32[]{:S(2)}) async-start(bf16[16,2,8192]{2,1,0:T(2,128)(2,1)} %reshape.824), calls=%async_computation.4 | async-start | bytes 1048576 | tf_op jit(solution)/shard_map/all_to_all | solution.py:32
  105.5 0.8 copy-start.1
  105.5 0.8 copy-start.2
  107.4 1.3 %copy-start.3 = (f32[1,32]{1,0:T(1,128)S(1)}, f32[1,32]{1,0:T(1,128)}, u32[]{:S(2)}) copy-start(f32[1,32]{1,0:T(1,128)} %param.11) | copy-start | bytes 388
  107.4 1.3 %copy-start.4 = (f32[1,32]{1,0:T(1,128)S(1)}, f32[1,32]{1,0:T(1,128)}, u32[]{:S(2)}) copy-start(f32[1,32]{1,0:T(1,128)} %param.10) | copy-start | bytes 388
where the time goes:
time: 120 us; the launch traced here: 119 us
  waiting for transfers between devices  34.7 us (29%)
  starting transfers between devices  27.6 us (23%)
  local copies, waits for them, and re-layouts  23.2 us (19%)
  other arithmetic  12.9 us (11%)
  matrix products  12.8 us (11%)
  blocking collectives  7.8 us (6%)
    all_to_all x2, waiting for transfers between devices, copy_for_each(): return lax.all_to_all(copies, axis, split_axis=0, concat_axis=0, tiled=True)  23.4 us
    unnamed x23, local copies, waits for them, and re-layouts  17 us
    all_to_all x2, starting transfers between devices, summed_on_arrival(): lax.all_to_all(cut_along(shard, dim, length), axis, 0, 0, tiled=True)  16.1 us
    all_to_all x2, starting transfers between devices, copy_for_each(): return lax.all_to_all(copies, axis, split_axis=0, concat_axis=0, tiled=True)  11.5 us
    all_to_all x2, waiting for transfers between devices, summed_on_arrival(): lax.all_to_all(cut_along(shard, dim, length), axis, 0, 0, tiled=True)  11.3 us
    broadcast_in_dim x1, other arithmetic, local(): return hidden[None]  10.6 us
    all_to_all x1, blocking collectives, copy_for_each(): return lax.all_to_all(copies, axis, split_axis=0, concat_axis=0, tiled=True)  7.8 us
    dot_general x4, matrix products, contract(): jnp.einsum('abcz,abcdz->abdz', left, right, preferred_element_type=jnp.fl...  3.09 us
  transfers between devices with their start and end apart: 4, of which 4 were waited for; matrix products, arithmetic and copies ran while one was open for 3% of the time, Pallas kernels for 0%

commit v1 on v0

v1 whole, which is shorter than its diff:
```python
import math

import jax
import jax.numpy as jnp
import numpy as np
from jax import lax
from jax.experimental import pallas as pl
from jax.experimental.pallas import tpu as pltpu
from jax.sharding import PartitionSpec as P

X = 128
Y = 128
Z = 128
MX = 16
MY = 16
MZ = 16
C = 32
TX = 8
TY = 32
YH = 4
YL = 8
KB = 4
KL = 4

norm_eps = 1e-05


def signed(count):
    index = np.arange(count)
    return np.where(index < count // 2, index, index - count)


def depth_table():
    phase = 2.0 * np.pi * ((np.arange(Z)[:, None] * np.arange(MZ)[None, :]) % Z) / Z
    parts = np.stack([np.cos(phase), -np.sin(phase)], axis=1)
    full = np.einsum("zrk,ab->azrbk", parts, np.eye(YL))
    return full.reshape(YL * Z, 2 * YL * MZ)


def second_table():
    cells = np.arange(TY)
    phase = 2.0 * np.pi * ((cells[:, None] * signed(MY)[None, :]) % Y) / Y
    cosine, sine = np.cos(phase), np.sin(phase)
    from_real = np.stack([cosine, -sine], axis=-1)
    from_imag = np.stack([sine, cosine], axis=-1)
    both = np.stack([from_real, from_imag], axis=1)
    both = both.reshape(YH, YL, 2, KB, KL, 2)
    full = np.einsum("hlrbkt,vw->hrlvbtkw", both, np.eye(MZ))
    return full.reshape(YH * 2 * YL * MZ, KB * 2 * KL * MZ)


def first_tables():
    cells = np.arange(TX)
    phase = 2.0 * np.pi * ((signed(MX)[:, None] * cells[None, :]) % X) / X
    cosine = np.kron(np.cos(phase), np.eye(C))
    sine = np.kron(np.sin(phase), np.eye(C))
    forward = np.concatenate([cosine, -sine], axis=1)
    backward = np.concatenate([cosine.T, sine.T], axis=0)
    return forward, backward


def turned(value):
    lane = lax.broadcasted_iota(jnp.int32, (1, 128), 1)
    sign = jnp.where(lane < 64, -1.0, 1.0)
    parts = [
        pltpu.roll(value[:, at : at + 128], 64, 1) * sign for at in range(0, value.shape[1], 128)
    ]
    return parts[0] if len(parts) == 1 else jnp.concatenate(parts, axis=1)


def dot(left, right):
    return jnp.dot(left, right, preferred_element_type=jnp.float32)


def dot_nt(left, right):
    return lax.dot_general(
        left, right, (((1,), (1,)), ((), ())), preferred_element_type=jnp.float32
    )


def forward_kernel(fields, depth, second, first, out):
    amplitude = None
    for p in range(YL // 2):
        left = jnp.concatenate(
            [fields[:, :, 2 * p + h].reshape(TX * YH * C, Z) for h in range(2)], axis=1
        )
        term = dot(left, depth[p * 2 * Z : (p + 1) * 2 * Z, :])
        amplitude = term if amplitude is None else amplitude + term
    amplitude = amplitude.astype(jnp.bfloat16).reshape(TX, YH, C, 2 * YL * MZ)
    along = None
    for h in range(YH):
        term = dot(amplitude[:, h].reshape(TX * C, 256), second[h * 256 : (h + 1) * 256, :])
        along = term if along is None else along + term
    both = jnp.concatenate(
        [along.astype(jnp.bfloat16), turned(along).astype(jnp.bfloat16)], axis=0
    )
    modes = dot(first[...], both).astype(jnp.bfloat16)
    for b in range(KB):
        out[:, b] = modes[:, b * 128 : (b + 1) * 128].reshape(MX, C, 128)


def mix_kernel(parts, weight, cosine, sine, spread, out):
    real = jnp.zeros((C, 128), jnp.float32)
    imag = jnp.zeros((C, 128), jnp.float32)
    for s in range(64):
        part = parts[s].astype(jnp.float32)
        real = real + part * cosine[s : s + 1, :]
        imag = imag + part * sine[s : s + 1, :]
    total = (real - turned(imag)) * (1.0 / math.sqrt(X * Y * Z))
    spectrum = dot(spread[...], total.astype(jnp.bfloat16))
    swapped = pltpu.roll(spectrum, 64, 1)
    lane = lax.broadcasted_iota(jnp.int32, (8, 128), 1)
    row = lax.broadcasted_iota(jnp.int32, (8, 128), 0)
    pieces = []
    for b in range(8):
        w = weight[b].astype(jnp.float32)
        same = jnp.sum((spectrum * w).reshape(16, 8, 128), axis=0)
        cross = jnp.sum((swapped * w).reshape(16, 8, 128), axis=0)
        same = same + pltpu.roll(same, 4, 0)
        cross = cross + pltpu.roll(cross, 4, 0)
        same = same - pltpu.roll(same, 64, 1)
        cross = cross + pltpu.roll(cross, 64, 1)
        pieces.append(jnp.where(lane < 64, same, cross))
    mixed = jnp.concatenate(
        [jnp.where(row < 4, pieces[2 * i], pieces[2 * i + 1]) for i in range(4)], axis=0
    )
    mixed_turned = turned(mixed)
    for s in range(64):
        out[s] = (mixed * cosine[s : s + 1, :] + mixed_turned * sine[s : s + 1, :]).astype(
            jnp.bfloat16
        )


def inverse_kernel(
    modes, fields, depth, second, first, skip, bias, gain, shift, out, rows, spectral
):
    h = pl.program_id(0)

    @pl.when(h == 0)
    def _():
        full = jnp.concatenate([modes[:, b].reshape(MX * C, 128) for b in range(KB)], axis=1)
        both = dot(first[...], full)
        lines = both[: TX * C] + turned(both[TX * C :])
        lines = (lines * (1.0 / math.sqrt(MX * MY * MZ))).astype(jnp.bfloat16)
        for i in range(YH):
            rows[i] = dot_nt(lines, second[i * 256 : (i + 1) * 256, :]).astype(jnp.bfloat16)

    spectral[...] = dot_nt(rows[h], depth[...])
    for x in range(0, TX, 2):
        cells = jnp.concatenate(
            [fields[x + i, 0].reshape(YL * C, Z) for i in range(2)], axis=1
        )
        skipped = dot(skip[...], cells)
        for i in range(2):
            for y in range(YL):
                pre = (
                    spectral[(x + i) * C : (x + i + 1) * C, y * Z : (y + 1) * Z]
                    + skipped[y * C : (y + 1) * C, i * Z : (i + 1) * Z]
                    + bias[...]
                )
                centre = jnp.sum(pre, axis=0, keepdims=True) * (1.0 / C)
                pre = pre - centre
                spread = jnp.sum(pre * pre, axis=0, keepdims=True) * (1.0 / C)
                normed = pre * lax.rsqrt(spread + norm_eps) * gain[...] + shift[...]
                half = normed * 0.5
                value = half * lax.erf(normed * math.sqrt(0.5)) + half
                out[x + i, 0, y] = value.astype(jnp.bfloat16)


def local(fields, spectral, skip_weight, skip_bias, norm_gain, norm_shift):
    bf16 = jnp.bfloat16
    hidden = fields.reshape(TX, YH, YL, C, Z)
    depth = jnp.asarray(depth_table(), bf16)
    second = jnp.asarray(second_table(), bf16)
    first_forward, first_backward = first_tables()
    first_forward = jnp.asarray(first_forward, bf16)
    first_backward = jnp.asarray(first_backward, bf16)
    spread = jnp.asarray(np.kron(np.eye(C), np.ones((4, 1))), bf16)

    weight = spectral[0, 0].transpose(2, 3, 1, 0, 4).reshape(128, 128)
    weight = lax.all_to_all(
        jnp.broadcast_to(weight, (8, 128, 128)), "col", split_axis=0, concat_axis=0, tiled=True
    )

    modes = pl.pallas_call(
        forward_kernel,
        out_shape=jax.ShapeDtypeStruct((MX, KB, C, 128), bf16),
        name="forward",
    )(hidden, depth, second, first_forward)
    parts = lax.all_to_all(
        modes.reshape(64, C, 128), ("gx", "gy"), split_axis=0, concat_axis=0, tiled=True
    )

    freq = jnp.arange(16, dtype=jnp.int32)
    freq = jnp.where(freq < 8, freq, freq - 16)
    at_x = lax.axis_index("gx").astype(jnp.int32)
    at_y = lax.axis_index("gy").astype(jnp.int32)
    freq_x = jnp.where(at_x < 8, at_x, at_x - 16)
    lane = lax.broadcasted_iota(jnp.int32, (64, 128), 1)
    place = lax.broadcasted_iota(jnp.int32, (64, 128), 0)
    freq_y = at_y * KL + lane // MZ % KL
    freq_y = jnp.where(freq_y < 8, freq_y, freq_y - 16)
    turn = (freq_x * (place // 4) + freq_y * (place % 4) * 4) % 16
    phase = turn.astype(jnp.float32) * (2.0 * math.pi / 16)
    mixed = pl.pallas_call(
        mix_kernel,
        out_shape=jax.ShapeDtypeStruct((64, C, 128), bf16),
        name="mix",
    )(parts, weight, jnp.cos(phase), jnp.sin(phase), spread)
    full = lax.all_to_all(mixed, ("gx", "gy"), split_axis=0, concat_axis=0, tiled=True)

    skip = jnp.kron(jnp.eye(8, dtype=bf16), skip_weight[0])
    column = lambda v: jnp.broadcast_to(v[0][:, None], (C, Z))
    whole = lambda shape: pl.BlockSpec(shape, lambda h: (0,) * len(shape))
    tile = pl.BlockSpec((TX, 1, YL, C, Z), lambda h: (0, h, 0, 0, 0))
    result = pl.pallas_call(
        inverse_kernel,
        grid=(YH,),
        in_specs=[
            whole((MX, KB, C, 128)),
            tile,
            whole((YL * Z, 256)),
            whole((YH * 256, 512)),
            whole((2 * TX * C, MX * C)),
            whole((256, 256)),
            whole((C, Z)),
            whole((C, Z)),
            whole((C, Z)),
        ],
        out_specs=tile,
        out_shape=jax.ShapeDtypeStruct((TX, YH, YL, C, Z), bf16),
        scratch_shapes=[
            pltpu.VMEM((YH, TX * C, 256), bf16),
            pltpu.VMEM((TX * C, YL * Z), jnp.float32),
        ],
        name="inverse",
    )(
        full.reshape(MX, KB, C, 128),
        hidden,
        depth,
        second,
        first_backward,
        skip,
        column(skip_bias),
        column(norm_gain),
        column(norm_shift),
    )
    return result.reshape(1, TX, TY, C, Z)


def solution(mesh):
    placed = (
        P("col", "gx", "gy", None, None),
        P(None, "gx", "gy", None, None, "col", None),
        P(),
        P(),
        P(),
        P(),
    )
    return jax.shard_map(
        local,
        mesh=mesh,
        in_specs=placed,
        out_specs=P("col", "gx", "gy", None, None),
        check_vma=False,
    )
```

time: 120 us -> 87.5 us (0.73)
  the two profiles are of different devices: /device:TPU:24 before, /device:TPU:8 now
where the time goes in v1:
time: 87.5 us; the launch traced here: 87 us
  waiting for transfers between devices  35.8 us (41%)
  starting transfers between devices  28 us (32%)
  Pallas kernels  15.8 us (18%)
  local copies, waits for them, and re-layouts  6.16 us (7%)
  other arithmetic  1.03 us (1%)
    all_to_all x1, waiting for transfers between devices, local(): lax.all_to_all(mixed, ('gx', 'gy'), split_axis=0, concat_axis=0, tiled=True)  14.8 us
    all_to_all x1, starting transfers between devices, local(): lax.all_to_all(modes.reshape(64, C, 128), ('gx', 'gy'), split_axis=0, con...  14.8 us
    all_to_all x1, waiting for transfers between devices, local(): lax.all_to_all(modes.reshape(64, C, 128), ('gx', 'gy'), split_axis=0, con...  13.6 us
    pallas_call x1, Pallas kernels, local(): pl.pallas_call(inverse_kernel, grid=(YH,), in_specs=[whole((MX, KB, C, 12...  7.86 us
    all_to_all x1, waiting for transfers between devices, local(): lax.all_to_all(jnp.broadcast_to(weight, (8, 128, 128)), 'col', split_axis...  7.38 us
    all_to_all x1, starting transfers between devices, local(): lax.all_to_all(mixed, ('gx', 'gy'), split_axis=0, concat_axis=0, tiled=True)  6.98 us
    all_to_all x1, starting transfers between devices, local(): lax.all_to_all(jnp.broadcast_to(weight, (8, 128, 128)), 'col', split_axis...  6.2 us
    pallas_call x1, Pallas kernels, local(): pl.pallas_call(forward_kernel, out_shape=jax.ShapeDtypeStruct((MX, KB, C,...  5.34 us
  transfers between devices with their start and end apart: 3, of which 3 were waited for; matrix products, arithmetic and copies ran while one was open for 2% of the time, Pallas kernels for 6%

profile of v1, /device:TPU:8, one launch (start us, length us, event | category | flops | bytes accessed | tf_op | source)
XLA Modules:
  0.0 87.0 jit_solution(16327553805281553248)
XLA Ops:
  0.0 1.3 %copy.12 = bf16[32,4,2,4,16]{4,3,2,1,0:T(4,128)(2,1)S(1)} copy(bf16[32,4,2,4,16]{0,4,1,2,3:T(8,128)(2,1)} %bitcast.17) | data formatting | bytes 65536 | tf_op jit(solution)/shard_map/transpose | solution.py:180
  1.3 0.2 reshape.35
  1.5 0.7 broadcast_in_dim.28
  2.3 6.2 %all-to-all-start.1 = ((bf16[8,128,128]{2,1,0:T(8,128)(2,1)}), bf16[8,128,128]{2,1,0:T(8,128)(2,1)S(1)}, u32[]{:S(2)}, u32[]{:S(2)}) async-start(bf16[8,128,128]{2,1,0:T(8,128)(2,1)} %broadcast_in_dim.28), calls=%async_computation.1 | async-start | bytes 524288 | tf_op jit(solution)/shard_map/all_to_all | solution.py:181
  8.5 5.3 %forward.1 = bf16[16,4,32,128]{3,2,1,0:T(8,128)(2,1)} custom-call(bf16[8,4,8,32,128]{4,3,2,1,0:T(8,128)(2,1)} %bitcast.13, bf16[1024,256]{1,0:T(8,128)(2,1)} %constant.92.clone.depth, bf16[1024,512]{1,0:T(8,128)(2,1)} %constant.93.clone.second, bf16[512,512]{1,0:T(8,128)(2,1)} %constant.94.clone.first), custom_call_target="tpu_custom_call" | custom-call | tf_op jit(solution)/shard_map/forward/pallas_call | solution.py:185
  13.8 7.4 %all-to-all-done.1.weight = bf16[8,128,128]{2,1,0:T(8,128)(2,1)S(1)} async-done(((bf16[8,128,128]{2,1,0:T(8,128)(2,1)}), bf16[8,128,128]{2,1,0:T(8,128)(2,1)S(1)}, u32[]{:S(2)}, u32[]{:S(2)}) %all-to-all-start.1) | async-done | bytes 262176 | tf_op jit(solution)/shard_map/all_to_all | solution.py:181
  21.2 14.8 %all-to-all-start = ((bf16[64,32,128]{2,1,0:T(8,128)(2,1)}), bf16[64,32,128]{2,1,0:T(8,128)(2,1)S(1)}, u32[]{:S(2)}, u32[]{:S(2)}) async-start(bf16[64,32,128]{2,1,0:T(8,128)(2,1)} %bitcast.15), calls=%async_computation | async-start | bytes 1048576 | tf_op jit(solution)/shard_map/all_to_all | solution.py:190
  36.0 0.0 copy-start.4
  36.0 0.0 copy-start.5
  36.0 0.0 copy-start.6
  36.1 0.9 %fusion.8 = (f32[64,128]{1,0:T(8,128)}, f32[64,128]{1,0:T(8,128)}) fusion(s32[64]{0:T(128)S(1)} %get-tuple-element.12, s32[64]{0:T(128)S(1)} %get-tuple-element.13, pred[64]{0:T(512)(128)(4,1)S(1)} %get-tuple-element.7, s32[128]{0:T(128)S(1)} %get-tuple-element.9, s32[128]{0:T(128)S(1)} %get-tuple-element.10, pred[128]{0:T(512)(128)(4,1)S(1)} %compare_and_fusion.1, ...), kind=kLoop, calls=%fused_computation.18 | loop fusion | flops 286720 | bytes 67848 | tf_op jit(solution)/shard_map/sin | solution.py:209
  37.0 13.6 %all-to-all-done.parts = bf16[64,32,128]{2,1,0:T(8,128)(2,1)S(1)} async-done(((bf16[64,32,128]{2,1,0:T(8,128)(2,1)}), bf16[64,32,128]{2,1,0:T(8,128)(2,1)S(1)}, u32[]{:S(2)}, u32[]{:S(2)}) %all-to-all-start) | async-done | bytes 524320 | tf_op jit(solution)/shard_map/all_to_all | solution.py:190
  50.7 0.0 copy-done.2
  50.7 0.8 copy-done
  51.4 2.6 %mix.1 = bf16[64,32,128]{2,1,0:T(8,128)(2,1)} custom-call(bf16[64,32,128]{2,1,0:T(8,128)(2,1)} %copy-done, bf16[8,128,128]{2,1,0:T(8,128)(2,1)} %copy-done.2, f32[64,128]{1,0:T(8,128)} %get-tuple-element.6.cosine, f32[64,128]{1,0:T(8,128)} %get-tuple-element.5.sine, bf16[128,32]{1,0:T(8,128)(2,1)} %constant.96.clone.spread), custom_call_target="tpu_custom_call" | custom-call | tf_op jit(solution)/shard_map/mix/pallas_call | solution.py:205
  54.1 7.0 %all-to-all-start.2 = ((bf16[64,32,128]{2,1,0:T(8,128)(2,1)}), bf16[64,32,128]{2,1,0:T(8,128)(2,1)S(1)}, u32[]{:S(2)}, u32[]{:S(2)}) async-start(bf16[64,32,128]{2,1,0:T(8,128)(2,1)} %mix.1), calls=%async_computation.2 | async-start | bytes 1048576 | tf_op jit(solution)/shard_map/all_to_all | solution.py:210
  61.1 0.1 broadcast_multiply_fusion
  61.2 1.0 %mul.59.skip = bf16[256,256]{1,0:T(8,128)(2,1)} reshape(bf16[8,32,8,32]{3,2,1,0:T(8,128)(2,1)S(1)} %broadcast_multiply_fusion) | data formatting | bytes 262144 | tf_op jit(solution)/shard_map/jit(kron)/mul | solution.py:212
  62.2 14.8 %all-to-all-done.2 = bf16[64,32,128]{2,1,0:T(8,128)(2,1)S(1)} async-done(((bf16[64,32,128]{2,1,0:T(8,128)(2,1)}), bf16[64,32,128]{2,1,0:T(8,128)(2,1)S(1)}, u32[]{:S(2)}, u32[]{:S(2)}) %all-to-all-start.2) | async-done | bytes 524320 | tf_op jit(solution)/shard_map/all_to_all | solution.py:210
  77.1 0.7 broadcast_in_dim.30.bias
  77.8 0.7 broadcast_in_dim.32.gain
  78.5 0.0 copy-done.6
  78.5 0.7 broadcast_in_dim.34.shift
  79.2 7.9 %inverse.1 = bf16[8,4,8,32,128]{4,3,2,1,0:T(8,128)(2,1)} custom-call(bf16[16,4,32,128]{3,2,1,0:T(8,128)(2,1)} %bitcast.16, bf16[8,4,8,32,128]{4,3,2,1,0:T(8,128)(2,1)} %bitcast.14, bf16[1024,256]{1,0:T(8,128)(2,1)} %constant.92.clone.depth, bf16[1024,512]{1,0:T(8,128)(2,1)} %constant.93.clone.second, bf16[512,512]{1,0:T(8,128)(2,1)} %constant.95.clone.first, ...), custom_call_target="tpu_custom_call" | custom-call | tf_op jit(solution)/shard_map/inverse/pallas_call | solution.py:216
  (14 shorter events, 0.0 us)
Async XLA Ops:
  2.3 18.9 %all-to-all-start.1 = ((bf16[8,128,128]{2,1,0:T(8,128)(2,1)}), bf16[8,128,128]{2,1,0:T(8,128)(2,1)S(1)}, u32[]{:S(2)}, u32[]{:S(2)}) async-start(bf16[8,128,128]{2,1,0:T(8,128)(2,1)} %broadcast_in_dim.28), calls=%async_computation.1 | async-start | bytes 524288 | tf_op jit(solution)/shard_map/all_to_all | solution.py:181
  13.8 47.3 %copy-start.3 = (bf16[1,32,32]{2,1,0:T(8,128)(2,1)S(1)}, bf16[1,32,32]{2,1,0:T(8,128)(2,1)}, u32[]{:S(2)}) copy-start(bf16[1,32,32]{2,1,0:T(8,128)(2,1)} %param.13) | copy-start | bytes 6148
  21.2 29.5 %copy-start.2 = (bf16[8,128,128]{2,1,0:T(8,128)(2,1)}, bf16[8,128,128]{2,1,0:T(8,128)(2,1)S(1)}, u32[]{:S(2)}) copy-start(bf16[8,128,128]{2,1,0:T(8,128)(2,1)S(1)} %all-to-all-done.1.weight) | copy-start | bytes 786436
  21.2 29.5 %all-to-all-start = ((bf16[64,32,128]{2,1,0:T(8,128)(2,1)}), bf16[64,32,128]{2,1,0:T(8,128)(2,1)S(1)}, u32[]{:S(2)}, u32[]{:S(2)}) async-start(bf16[64,32,128]{2,1,0:T(8,128)(2,1)} %bitcast.15), calls=%async_computation | async-start | bytes 1048576 | tf_op jit(solution)/shard_map/all_to_all | solution.py:190
  36.0 41.1 %copy-start.4 = (f32[1,32]{1,0:T(1,128)S(1)}, f32[1,32]{1,0:T(1,128)}, u32[]{:S(2)}) copy-start(f32[1,32]{1,0:T(1,128)} %param.14) | copy-start | bytes 388
  36.0 41.8 %copy-start.5 = (f32[1,32]{1,0:T(1,128)S(1)}, f32[1,32]{1,0:T(1,128)}, u32[]{:S(2)}) copy-start(f32[1,32]{1,0:T(1,128)} %param.15) | copy-start | bytes 388
  36.0 42.4 %copy-start.6 = (f32[1,32]{1,0:T(1,128)S(1)}, f32[1,32]{1,0:T(1,128)}, u32[]{:S(2)}) copy-start(f32[1,32]{1,0:T(1,128)} %param.16) | copy-start | bytes 388
  50.6 0.8 copy-start
  54.1 23.0 %all-to-all-start.2 = ((bf16[64,32,128]{2,1,0:T(8,128)(2,1)}), bf16[64,32,128]{2,1,0:T(8,128)(2,1)S(1)}, u32[]{:S(2)}, u32[]{:S(2)}) async-start(bf16[64,32,128]{2,1,0:T(8,128)(2,1)} %mix.1), calls=%async_computation.2 | async-start | bytes 1048576 | tf_op jit(solution)/shard_map/all_to_all | solution.py:210
  77.1 2.1 %copy-start.1 = (bf16[64,32,128]{2,1,0:T(8,128)(2,1)}, bf16[64,32,128]{2,1,0:T(8,128)(2,1)S(1)}, u32[]{:S(2)}) copy-start(bf16[64,32,128]{2,1,0:T(8,128)(2,1)S(1)} %all-to-all-done.2) | copy-start | bytes 1572868

commit v2 on v1

v2 whole, which is shorter than its diff:
```python
import math

import jax
import jax.numpy as jnp
import numpy as np
from jax import lax
from jax.experimental import pallas as pl
from jax.experimental.pallas import tpu as pltpu
from jax.sharding import PartitionSpec as P


X = 128
Y = 128
Z = 128
MX = 16
MY = 16
MZ = 16
C = 32
TX = 8
TY = 32
YH = 4
YL = 8
KB = 4
KL = 4

norm_eps = 1e-05


def signed(count):
    index = np.arange(count)
    return np.where(index < count // 2, index, index - count)


def depth_table():
    phase = 2.0 * np.pi * ((np.arange(Z)[:, None] * np.arange(MZ)[None, :]) % Z) / Z
    parts = np.stack([np.cos(phase), -np.sin(phase)], axis=1)
    full = np.einsum("zrk,ab->azrbk", parts, np.eye(YL))
    return full.reshape(YL * Z, 2 * YL * MZ)


def second_table():
    cells = np.arange(TY)
    phase = 2.0 * np.pi * ((cells[:, None] * signed(MY)[None, :]) % Y) / Y
    cosine, sine = np.cos(phase), np.sin(phase)
    from_real = np.stack([cosine, -sine], axis=-1)
    from_imag = np.stack([sine, cosine], axis=-1)
    both = np.stack([from_real, from_imag], axis=1)
    both = both.reshape(YH, YL, 2, KB, KL, 2)
    full = np.einsum("hlrbkt,vw->hrlvbtkw", both, np.eye(MZ))
    return full.reshape(YH * 2 * YL * MZ, KB * 2 * KL * MZ)


def first_tables():
    cells = np.arange(TX)
    phase = 2.0 * np.pi * ((signed(MX)[:, None] * cells[None, :]) % X) / X
    cosine = np.kron(np.cos(phase), np.eye(C))
    sine = np.kron(np.sin(phase), np.eye(C))
    forward = np.concatenate([cosine, -sine], axis=1)
    backward = np.concatenate([cosine.T, sine.T], axis=0)
    return forward, backward


def turned(value):
    lane = lax.broadcasted_iota(jnp.int32, (1, 128), 1)
    sign = jnp.where(lane < 64, -1.0, 1.0)
    parts = [
        pltpu.roll(value[:, at : at + 128], 64, 1) * sign for at in range(0, value.shape[1], 128)
    ]
    return parts[0] if len(parts) == 1 else jnp.concatenate(parts, axis=1)


def dot(left, right):
    return jnp.dot(left, right, preferred_element_type=jnp.float32)


def dot_nt(left, right):
    return lax.dot_general(
        left, right, (((1,), (1,)), ((), ())), preferred_element_type=jnp.float32
    )


def forward_kernel(
    fields_far, depth_far, second_far, first_far, out, fields, depth, second, first, sems
):
    half = TX // 2
    pairs = [
        (depth_far, depth),
        (fields_far.at[:half], fields.at[:half]),
        (fields_far.at[half:], fields.at[half:]),
        (second_far, second),
        (first_far, first),
    ]
    copies = [
        pltpu.make_async_copy(here, there, sems.at[n]) for n, (here, there) in enumerate(pairs)
    ]
    for copy in copies:
        copy.start()
    copies[0].wait()
    amplitudes = []
    for part in range(2):
        copies[1 + part].wait()
        amplitude = None
        for p in range(YL // 2):
            left = jnp.concatenate(
                [
                    fields[part * half : (part + 1) * half, :, 2 * p + h].reshape(-1, Z)
                    for h in range(2)
                ],
                axis=1,
            )
            term = dot(left, depth[p * 2 * Z : (p + 1) * 2 * Z, :])
            amplitude = term if amplitude is None else amplitude + term
        amplitudes.append(amplitude.astype(jnp.bfloat16).reshape(half, YH, C, 2 * YL * MZ))
    amplitude = jnp.concatenate(amplitudes, axis=0)
    copies[3].wait()
    along = None
    for h in range(YH):
        term = dot(amplitude[:, h].reshape(TX * C, 256), second[h * 256 : (h + 1) * 256, :])
        along = term if along is None else along + term
    both = jnp.concatenate(
        [along.astype(jnp.bfloat16), turned(along).astype(jnp.bfloat16)], axis=0
    )
    copies[4].wait()
    modes = dot(first[...], both).astype(jnp.bfloat16)
    for b in range(KB):
        for j in range(MX):
            out[j * KB + b] = modes[j * C : (j + 1) * C, b * 128 : (b + 1) * 128]


def prepare_kernel(spectral, out):
    row = lax.broadcasted_iota(jnp.int32, (4 * C, C), 0)
    column = lax.broadcasted_iota(jnp.int32, (4 * C, C), 1)
    total = jnp.zeros((4 * C, 128), jnp.float32)
    for d in range(4):
        piece = jnp.concatenate(
            [spectral[k, r, d] for r in range(2) for k in range(KL)], axis=0
        )
        pick = jnp.where(row == column * 4 + d, 1.0, 0.0).astype(jnp.bfloat16)
        total = total + dot_nt(pick, piece)
    weight = total.astype(jnp.bfloat16)
    for i in range(4):
        out[i] = weight


def position_phases():
    at_x = lax.axis_index("gx").astype(jnp.int32)
    at_y = lax.axis_index("gy").astype(jnp.int32)
    freq_x = jnp.where(at_x < 8, at_x, at_x - 16)
    lane = lax.broadcasted_iota(jnp.int32, (64, 128), 1)
    place = lax.broadcasted_iota(jnp.int32, (64, 128), 0)
    freq_y = at_y * KL + ((lane >> 4) & 3)
    freq_y = jnp.where(freq_y < 8, freq_y, freq_y - 16)
    turn = (freq_x * (place >> 2) + freq_y * (place & 3) * 4) & 15
    cosine = jnp.ones((64, 128), jnp.float32)
    sine = jnp.zeros((64, 128), jnp.float32)
    for n in range(1, 16):
        here = turn == n
        cosine = jnp.where(here, math.cos(2.0 * math.pi * n / 16), cosine)
        sine = jnp.where(here, math.sin(2.0 * math.pi * n / 16), sine)
    return cosine, sine


def collect_kernel(parts, second_far, back_far, out, second, back, cosine, sine, sems):
    copies = [
        pltpu.make_async_copy(second_far, second, sems.at[0]),
        pltpu.make_async_copy(back_far, back, sems.at[1]),
    ]
    for copy in copies:
        copy.start()
    cosine[...], sine[...] = position_phases()
    real = jnp.zeros((C, 128), jnp.float32)
    imag = jnp.zeros((C, 128), jnp.float32)
    for s in range(64):
        part = parts[s].astype(jnp.float32)
        real = real + part * cosine[s : s + 1, :]
        imag = imag + part * sine[s : s + 1, :]
    total = (real - turned(imag)) * (1.0 / math.sqrt(X * Y * Z))
    out[...] = total
    for copy in copies:
        copy.wait()


def mix_kernel(total, near, far, cosine, sine, out):
    row = lax.broadcasted_iota(jnp.int32, (4 * C, C), 0)
    column = lax.broadcasted_iota(jnp.int32, (4 * C, C), 1)
    repeat = jnp.where((row >> 2) == column, 1.0, 0.0).astype(jnp.bfloat16)
    spectrum = dot(repeat, total[...].astype(jnp.bfloat16))
    swapped = pltpu.roll(spectrum, 64, 1)
    lane = lax.broadcasted_iota(jnp.int32, (8, 128), 1)
    row = lax.broadcasted_iota(jnp.int32, (8, 128), 0)

    def mixed_with(weight):
        w = weight.astype(jnp.float32)
        same = jnp.sum((spectrum * w).reshape(16, 8, 128), axis=0)
        cross = jnp.sum((swapped * w).reshape(16, 8, 128), axis=0)
        same = same + pltpu.roll(same, 4, 0)
        cross = cross + pltpu.roll(cross, 4, 0)
        same = same - pltpu.roll(same, 64, 1)
        cross = cross + pltpu.roll(cross, 64, 1)
        return jnp.where(lane < 64, same, cross)

    upper = lax.axis_index("col").astype(jnp.int32) & 1
    nearer = (row >> 2) == upper
    mixed = jnp.concatenate(
        [jnp.where(nearer, mixed_with(near[i]), mixed_with(far[i])) for i in range(4)], axis=0
    )
    mixed_turned = turned(mixed)
    for s in range(64):
        out[s] = (mixed * cosine[s : s + 1, :] + mixed_turned * sine[s : s + 1, :]).astype(
            jnp.bfloat16
        )


def column_of(vector):
    row = lax.broadcasted_iota(jnp.int32, (C, C), 0)
    column = lax.broadcasted_iota(jnp.int32, (C, C), 1)
    spread = jnp.where(row == column, jnp.broadcast_to(vector[...], (C, C)), 0.0)
    return jnp.broadcast_to(jnp.sum(spread, axis=1, keepdims=True), (C, Z))


def inverse_kernel(
    modes, fields, depth, second, first, skip, bias, gain, shift, out, rows, spectral, done, sems
):
    full = jnp.concatenate(
        [
            jnp.concatenate([modes[j * KB + b] for j in range(MX)], axis=0)
            for b in range(KB)
        ],
        axis=1,
    )
    both = dot(first[...], full)
    lines = both[: TX * C] + turned(both[TX * C :])
    lines = (lines * (1.0 / math.sqrt(MX * MY * MZ))).astype(jnp.bfloat16)
    rows[...] = dot_nt(lines, second[...]).astype(jnp.bfloat16)
    row = lax.broadcasted_iota(jnp.int32, (YL * C, YL * C), 0)
    column = lax.broadcasted_iota(jnp.int32, (YL * C, YL * C), 1)
    wide = jnp.concatenate([skip[0]] * YL, axis=1)
    tall = jnp.concatenate([wide] * YL, axis=0).astype(jnp.float32)
    skips = jnp.where((row >> 5) == (column >> 5), tall, 0.0).astype(jnp.bfloat16)
    bias = column_of(bias)
    gain = column_of(gain)
    shift = column_of(shift)
    copies = []
    for h in range(YH):
        spectral[h % 2] = dot_nt(rows[:, h * 256 : (h + 1) * 256], depth[...])
        for x in range(0, TX, 2):
            cells = jnp.concatenate(
                [fields[x + i, h].reshape(YL * C, Z) for i in range(2)], axis=1
            )
            skipped = dot(skips, cells)
            for i in range(2):
                for y in range(YL):
                    pre = (
                        spectral[h % 2, (x + i) * C : (x + i + 1) * C, y * Z : (y + 1) * Z]
                        + skipped[y * C : (y + 1) * C, i * Z : (i + 1) * Z]
                        + bias
                    )
                    centre = jnp.sum(pre, axis=0, keepdims=True) * (1.0 / C)
                    pre = pre - centre
                    spread = jnp.sum(pre * pre, axis=0, keepdims=True) * (1.0 / C)
                    normed = pre * lax.rsqrt(spread + norm_eps) * gain + shift
                    half = normed * 0.5
                    value = half * lax.erf(normed * math.sqrt(0.5)) + half
                    done[h, x + i, y] = value.astype(jnp.bfloat16)
        copy = pltpu.make_async_copy(done.at[h], out.at[:, h], sems.at[h])
        copy.start()
        copies.append(copy)
    for copy in copies:
        copy.wait()


def near(value):
    return pltpu.with_memory_space_constraint(value, pltpu.VMEM)


def far(value):
    return pltpu.with_memory_space_constraint(value, pltpu.HBM)


def local(fields, spectral, skip_weight, skip_bias, norm_gain, norm_shift):
    bf16 = jnp.bfloat16
    hidden = fields.reshape(TX, YH, YL, C, Z)
    depth = jnp.asarray(depth_table(), bf16)
    second = jnp.asarray(second_table(), bf16)
    first_forward, first_backward = first_tables()
    first_forward = jnp.asarray(first_forward, bf16)
    first_backward = jnp.asarray(first_backward, bf16)
    anywhere = pl.BlockSpec(memory_space=pl.ANY)

    weight = pl.pallas_call(
        prepare_kernel,
        out_shape=jax.ShapeDtypeStruct((4, 128, 128), bf16),
        compiler_params=pltpu.CompilerParams(vmem_limit_bytes=8 << 20),
        name="prepare",
    )(spectral[0, 0].transpose(0, 1, 3, 4, 2))
    own = lax.all_to_all(
        weight,
        "col",
        split_axis=0,
        concat_axis=0,
        axis_index_groups=[[0, 2, 4, 6], [1, 3, 5, 7]],
        tiled=True,
    )
    other = lax.ppermute(own, "col", [(i, i ^ 1) for i in range(8)])

    modes, hidden, depth = pl.pallas_call(
        forward_kernel,
        in_specs=[anywhere] * 4,
        out_shape=[
            pltpu.VMEM((64, C, 128), bf16),
            pltpu.VMEM(hidden.shape, bf16),
            pltpu.VMEM(depth.shape, bf16),
        ],
        scratch_shapes=[
            pltpu.VMEM(second.shape, bf16),
            pltpu.VMEM(first_forward.shape, bf16),
            pltpu.SemaphoreType.DMA((5,)),
        ],
        compiler_params=pltpu.CompilerParams(vmem_limit_bytes=20 << 20),
        name="forward",
    )(far(hidden), far(depth), far(second), far(first_forward))
    parts = lax.all_to_all(
        modes, ("gx", "gy"), split_axis=0, concat_axis=0, tiled=True
    )
    inside = pl.BlockSpec(memory_space=pltpu.VMEM)
    total, second, first_backward, cosine, sine = pl.pallas_call(
        collect_kernel,
        in_specs=[inside] + [anywhere] * 2,
        out_shape=[
            pltpu.VMEM((C, 128), jnp.float32),
            pltpu.VMEM(second.shape, bf16),
            pltpu.VMEM(first_backward.shape, bf16),
            pltpu.VMEM((64, 128), jnp.float32),
            pltpu.VMEM((64, 128), jnp.float32),
        ],
        scratch_shapes=[pltpu.SemaphoreType.DMA((2,))],
        compiler_params=pltpu.CompilerParams(vmem_limit_bytes=12 << 20),
        name="collect",
    )(near(parts), far(second), far(first_backward))
    mixed = pl.pallas_call(
        mix_kernel,
        out_shape=pltpu.VMEM((64, C, 128), bf16),
        compiler_params=pltpu.CompilerParams(vmem_limit_bytes=12 << 20),
        name="mix",
    )(total, near(own), near(other), cosine, sine)
    full = lax.all_to_all(mixed, ("gx", "gy"), split_axis=0, concat_axis=0, tiled=True)
    result = pl.pallas_call(
        inverse_kernel,
        out_shape=jax.ShapeDtypeStruct((TX, YH, YL, C, Z), bf16),
        out_specs=anywhere,
        scratch_shapes=[
            pltpu.VMEM((TX * C, YH * 256), bf16),
            pltpu.VMEM((2, TX * C, YL * Z), jnp.float32),
            pltpu.VMEM((YH, TX, YL, C, Z), bf16),
            pltpu.SemaphoreType.DMA((YH,)),
        ],
        compiler_params=pltpu.CompilerParams(vmem_limit_bytes=24 << 20),
        name="inverse",
    )(
        near(full),
        hidden,
        depth,
        second,
        first_backward,
        skip_weight,
        skip_bias,
        norm_gain,
        norm_shift,
    )
    return result.reshape(1, TX, TY, C, Z)


def solution(mesh):
    placed = (
        P("col", "gx", "gy", None, None),
        P(None, "gx", "gy", None, None, "col", None),
        P(),
        P(),
        P(),
        P(),
    )
    return jax.shard_map(
        local,
        mesh=mesh,
        in_specs=placed,
        out_specs=P("col", "gx", "gy", None, None),
        check_vma=False,
    )
```

time: 87.5 us -> 76 us (0.87)
  blocking collectives: 0 us -> 22.5 us
  waiting for transfers between devices: 35.8 us -> 16.5 us
  Pallas kernels: 15.8 us -> 11.3 us
  starting transfers between devices: 28 us -> 23.5 us
  local copies, waits for them, and re-layouts: 6.16 us -> 1.72 us
  other arithmetic: 1.03 us -> 0 us
    all_to_all x0 -> x1, blocking collectives: none -> 22.5 us  [local(): lax.all_to_all(mixed, ('gx', 'gy'), split_axis=0, concat_axis=0, tiled=True)]
    all_to_all x3 -> x2, waiting for transfers between devices: 35.8 us -> 16.5 us  [the longest x1 12.3 us: local(): lax.all_to_all(modes, ('gx', 'gy'), split_axis=0, concat_axis=0, tiled=True)]
    all_to_all x3 -> x2, starting transfers between devices: 28 us -> 21.4 us  [the longest x1 15.3 us: local(): lax.all_to_all(modes, ('gx', 'gy'), split_axis=0, concat_axis=0, tiled=True)]
    pallas_call x3 -> x5, Pallas kernels: 15.8 us -> 11.3 us  [the longest x1 4.72 us: local(): pl.pallas_call(inverse_kernel, out_shape=jax.ShapeDtypeStruct((TX, YH, YL...]
    broadcast_in_dim x4 -> x0, local copies, waits for them, and re-layouts: 2.81 us -> none  [the longest x3 2.08 us: local(): column = lambda v: jnp.broadcast_to(v[0][:, None], (C, Z))]
    ppermute x0 -> x1, starting transfers between devices: none -> 2.05 us  [local(): other = lax.ppermute(own, 'col', [(i, i ^ 1) for i in range(8)])]
    transpose x1 -> x0, local copies, waits for them, and re-layouts: 1.33 us -> none  [local(): weight = spectral[0, 0].transpose(2, 3, 1, 0, 4).reshape(128, 128)]
    mul x1 -> x0, local copies, waits for them, and re-layouts: 1.02 us -> none  [local(): skip = jnp.kron(jnp.eye(8, dtype=bf16), skip_weight[0])]
  transfers between devices with their start and end apart: 3 -> 3, of which waited for: 3 -> 2; matrix products, arithmetic and copies ran while one was open for 2% -> 0% of each run, Pallas kernels for 6% -> 7%
where the time goes in v2:
time: 76 us; the launch traced here: 75.6 us
  starting transfers between devices  23.5 us (31%)
  blocking collectives  22.5 us (30%)
  waiting for transfers between devices  16.5 us (22%)
  Pallas kernels  11.3 us (15%)
  local copies, waits for them, and re-layouts  1.72 us (2%)
    all_to_all x1, blocking collectives, local(): lax.all_to_all(mixed, ('gx', 'gy'), split_axis=0, concat_axis=0, tiled=True)  22.5 us
    all_to_all x1, starting transfers between devices, local(): lax.all_to_all(modes, ('gx', 'gy'), split_axis=0, concat_axis=0, tiled=True)  15.3 us
    all_to_all x1, waiting for transfers between devices, local(): lax.all_to_all(modes, ('gx', 'gy'), split_axis=0, concat_axis=0, tiled=True)  12.3 us
    all_to_all x1, starting transfers between devices, local(): lax.all_to_all(weight, 'col', split_axis=0, concat_axis=0, axis_index_gro...  6.19 us
    pallas_call x1, Pallas kernels, local(): pl.pallas_call(inverse_kernel, out_shape=jax.ShapeDtypeStruct((TX, YH, YL...  4.72 us
    all_to_all x1, waiting for transfers between devices, local(): lax.all_to_all(weight, 'col', split_axis=0, concat_axis=0, axis_index_gro...  4.18 us
    pallas_call x1, Pallas kernels, local(): pl.pallas_call(forward_kernel, in_specs=[anywhere] * 4, out_shape=[pltpu....  3.83 us
    ppermute x1, starting transfers between devices, local(): other = lax.ppermute(own, 'col', [(i, i ^ 1) for i in range(8)])  2.05 us
  transfers between devices with their start and end apart: 3, of which 2 were waited for; matrix products, arithmetic and copies ran while one was open for 0% of the time, Pallas kernels for 7%

profile of v2, /device:TPU:8, one launch (start us, length us, event | category | flops | bytes accessed | tf_op | source)
XLA Modules:
  0.0 75.6 jit_solution(6945917837566567825)
XLA Ops:
  0.0 0.0 copy-start.1
  0.0 0.9 %copy-done.1 = bf16[1,1,4,2,32,4,16]{4,6,5,3,2,1,0:T(8,128)(2,1)S(1)} copy-done((bf16[1,1,4,2,32,4,16]{4,6,5,3,2,1,0:T(8,128)(2,1)S(1)}, bf16[1,1,4,2,32,4,16]{4,6,5,3,2,1,0:T(8,128)(2,1)}, u32[]{:S(2)}) %copy-start.1) | copy-done | bytes 32792
  0.9 0.9 %prepare.1 = bf16[4,128,128]{2,1,0:T(8,128)(2,1)} custom-call(bf16[4,2,4,16,32]{4,3,2,1,0:T(8,128)(2,1)S(1)} %bitcast.5), custom_call_target="tpu_custom_call" | custom-call | tf_op jit(solution)/shard_map/prepare/pallas_call | solution.py:290
  1.8 6.2 %all-to-all-start.1 = ((bf16[4,128,128]{2,1,0:T(8,128)(2,1)}), bf16[4,128,128]{2,1,0:T(8,128)(2,1)S(1)}, u32[]{:S(2)}, u32[]{:S(2)}) async-start(bf16[4,128,128]{2,1,0:T(8,128)(2,1)} %prepare.1), calls=%async_computation.1 | async-start | bytes 262144 | tf_op jit(solution)/shard_map/all_to_all | solution.py:296
  8.0 3.8 %forward.1 = (bf16[64,32,128]{2,1,0:T(8,128)(2,1)S(1)}, bf16[8,4,8,32,128]{4,3,2,1,0:T(8,128)(2,1)S(1)}, bf16[1024,256]{1,0:T(8,128)(2,1)S(1)}) custom-call(bf16[8,4,8,32,128]{4,3,2,1,0:T(8,128)(2,1)} %bitcast.6, bf16[1024,256]{1,0:T(8,128)(2,1)} %constant.8.clone.depth_far, bf16[1024,512]{1,0:T(8,128)(2,1)} %constant.9.clone.second_far, ...), custom_call_target="tpu_custom_call" | custom-call | tf_op jit(solution)/shard_map/forward/pallas_call | solution.py:306
  11.8 0.0 copy-start
  11.8 0.8 %copy-done = bf16[64,32,128]{2,1,0:T(8,128)(2,1)} copy-done((bf16[64,32,128]{2,1,0:T(8,128)(2,1)}, bf16[64,32,128]{2,1,0:T(8,128)(2,1)S(1)}, u32[]{:S(2)}) %copy-start) | copy-done | bytes 524312
  12.6 4.2 %all-to-all-done.1.near = bf16[4,128,128]{2,1,0:T(8,128)(2,1)S(1)} async-done(((bf16[4,128,128]{2,1,0:T(8,128)(2,1)}), bf16[4,128,128]{2,1,0:T(8,128)(2,1)S(1)}, u32[]{:S(2)}, u32[]{:S(2)}) %all-to-all-start.1) | async-done | bytes 131104 | tf_op jit(solution)/shard_map/all_to_all | solution.py:296
  16.8 15.3 %all-to-all-start = ((bf16[64,32,128]{2,1,0:T(8,128)(2,1)}), bf16[64,32,128]{2,1,0:T(8,128)(2,1)S(1)}, u32[]{:S(2)}, u32[]{:S(2)}) async-start(bf16[64,32,128]{2,1,0:T(8,128)(2,1)} %copy-done), calls=%async_computation | async-start | bytes 1048576 | tf_op jit(solution)/shard_map/all_to_all | solution.py:322
  32.0 0.0 copy-start.2
  32.1 0.0 copy-start.3
  32.1 0.0 copy-start.4
  32.1 0.0 copy-start.5
  32.1 2.1 %collective-permute-start = (bf16[4,128,128]{2,1,0:T(8,128)(2,1)S(1)}, bf16[4,128,128]{2,1,0:T(8,128)(2,1)S(1)}, u32[]{:S(2)}, u32[]{:S(2)}) collective-permute-start(bf16[4,128,128]{2,1,0:T(8,128)(2,1)S(1)} %all-to-all-done.1.near), channel_id=1, source_target_pairs={{0,1},{1,0},{2,3},{3,2},{4,5},{5,4},{6,7},{7,6},{8,9},{9,8},{10,11... | collective-permute-start | bytes 393224 | tf_op jit(solution)/shard_map/ppermute | solution.py:304
  34.2 12.3 %all-to-all-done.parts = bf16[64,32,128]{2,1,0:T(8,128)(2,1)S(1)} async-done(((bf16[64,32,128]{2,1,0:T(8,128)(2,1)}), bf16[64,32,128]{2,1,0:T(8,128)(2,1)S(1)}, u32[]{:S(2)}, u32[]{:S(2)}) %all-to-all-start) | async-done | bytes 524320 | tf_op jit(solution)/shard_map/all_to_all | solution.py:322
  46.5 1.4 %collect.1 = (f32[32,128]{1,0:T(8,128)S(1)}, bf16[1024,512]{1,0:T(8,128)(2,1)S(1)}, bf16[512,512]{1,0:T(8,128)(2,1)S(1)}, f32[64,128]{1,0:T(8,128)S(1)}, f32[64,128]{1,0:T(8,128)S(1)}) custom-call(bf16[64,32,128]{2,1,0:T(8,128)(2,1)S(1)} %all-to-all-done.parts, bf16[1024,512]{1,0:T(8,128)(2,1)} %constant.9.clone.second_far, ...), custom_call_target="tpu_custom_call" | custom-call | tf_op jit(solution)/shard_map/collect/pallas_call | solution.py:326
  47.9 0.0 collective-permute-done.far
  47.9 0.5 mix.1
  48.4 22.5 %all_to_all.15.modes = bf16[64,32,128]{2,1,0:T(8,128)(2,1)S(1)} all-to-all(bf16[64,32,128]{2,1,0:T(8,128)(2,1)S(1)} %mix.1), channel_id=1, replica_groups=mesh['gx'=16,'gy'=4,'col'=8] {'gx','gy'}, dimensions={0} | all-to-all | bytes 1048576 | tf_op jit(solution)/shard_map/all_to_all | solution.py:346
  70.9 0.0 copy-done.2
  70.9 0.0 copy-done.3
  70.9 0.0 copy-done.4
  70.9 0.0 copy-done.5
  70.9 4.7 %inverse.1 = bf16[8,4,8,32,128]{4,3,2,1,0:T(8,128)(2,1)} custom-call(bf16[64,32,128]{2,1,0:T(8,128)(2,1)S(1)} %all_to_all.15.modes, bf16[8,4,8,32,128]{4,3,2,1,0:T(8,128)(2,1)S(1)} %get-tuple-element.17.fields, bf16[1024,256]{1,0:T(8,128)(2,1)S(1)} %get-tuple-element.18.depth, bf16[1024,512]{1,0:T(8,128)(2,1)S(1)} %get-tuple-element.19.second, ...), custom_call_target="tpu_custom_call" | custom-call | tf_op jit(solution)/shard_map/inverse/pallas_call | solution.py:347
Async XLA Ops:
  0.0 0.9 %copy-start.1 = (bf16[1,1,4,2,32,4,16]{4,6,5,3,2,1,0:T(8,128)(2,1)S(1)}, bf16[1,1,4,2,32,4,16]{4,6,5,3,2,1,0:T(8,128)(2,1)}, u32[]{:S(2)}) copy-start(bf16[1,1,4,2,32,4,16]{4,6,5,3,2,1,0:T(8,128)(2,1)} %param.11) | copy-start | bytes 98308
  1.8 15.0 %all-to-all-start.1 = ((bf16[4,128,128]{2,1,0:T(8,128)(2,1)}), bf16[4,128,128]{2,1,0:T(8,128)(2,1)S(1)}, u32[]{:S(2)}, u32[]{:S(2)}) async-start(bf16[4,128,128]{2,1,0:T(8,128)(2,1)} %prepare.1), calls=%async_computation.1 | async-start | bytes 262144 | tf_op jit(solution)/shard_map/all_to_all | solution.py:296
  11.8 0.8 %copy-start = (bf16[64,32,128]{2,1,0:T(8,128)(2,1)}, bf16[64,32,128]{2,1,0:T(8,128)(2,1)S(1)}, u32[]{:S(2)}) copy-start(bf16[64,32,128]{2,1,0:T(8,128)(2,1)S(1)} %get-tuple-element.13) | copy-start | bytes 1572868
  16.8 29.7 %all-to-all-start = ((bf16[64,32,128]{2,1,0:T(8,128)(2,1)}), bf16[64,32,128]{2,1,0:T(8,128)(2,1)S(1)}, u32[]{:S(2)}, u32[]{:S(2)}) async-start(bf16[64,32,128]{2,1,0:T(8,128)(2,1)} %copy-done), calls=%async_computation | async-start | bytes 1048576 | tf_op jit(solution)/shard_map/all_to_all | solution.py:322
  32.0 38.8 %copy-start.2 = (bf16[1,32,32]{2,1,0:T(8,128)(2,1)S(1)}, bf16[1,32,32]{2,1,0:T(8,128)(2,1)}, u32[]{:S(2)}) copy-start(bf16[1,32,32]{2,1,0:T(8,128)(2,1)} %skip.1) | copy-start | bytes 6148
  32.1 38.8 %copy-start.3 = (f32[1,32]{1,0:T(1,128)S(1)}, f32[1,32]{1,0:T(1,128)}, u32[]{:S(2)}) copy-start(f32[1,32]{1,0:T(1,128)} %bias.1) | copy-start | bytes 388
  32.1 38.8 %copy-start.4 = (f32[1,32]{1,0:T(1,128)S(1)}, f32[1,32]{1,0:T(1,128)}, u32[]{:S(2)}) copy-start(f32[1,32]{1,0:T(1,128)} %gain.1) | copy-start | bytes 388
  32.1 38.8 %copy-start.5 = (f32[1,32]{1,0:T(1,128)S(1)}, f32[1,32]{1,0:T(1,128)}, u32[]{:S(2)}) copy-start(f32[1,32]{1,0:T(1,128)} %shift.1) | copy-start | bytes 388
  32.1 15.8 %collective-permute-start = (bf16[4,128,128]{2,1,0:T(8,128)(2,1)S(1)}, bf16[4,128,128]{2,1,0:T(8,128)(2,1)S(1)}, u32[]{:S(2)}, u32[]{:S(2)}) collective-permute-start(bf16[4,128,128]{2,1,0:T(8,128)(2,1)S(1)} %all-to-all-done.1.near), channel_id=1, source_target_pairs={{0,1},{1,0},{2,3},{3,2},{4,5},{5,4},{6,7},{7,6},{8,9},{9,8},{10,11... | collective-permute-start | bytes 393224 | tf_op jit(solution)/shard_map/ppermute | solution.py:304

commit v3 on v2

--- a/solution.py
+++ b/solution.py
@@ -80,7 +80,7 @@
 
 
 def forward_kernel(
-    fields_far, depth_far, second_far, first_far, out, fields, depth, second, first, sems
+    fields_far, depth_far, second_far, first_far, out_far, fields, depth, second, first, out, sems
 ):
     half = TX // 2
     pairs = [
@@ -93,12 +93,13 @@
     copies = [
         pltpu.make_async_copy(here, there, sems.at[n]) for n, (here, there) in enumerate(pairs)
     ]
-    for copy in copies:
+    for copy in copies[:3]:
         copy.start()
     copies[0].wait()
     amplitudes = []
     for part in range(2):
         copies[1 + part].wait()
+        copies[3 + part].start()
         amplitude = None
         for p in range(YL // 2):
             left = jnp.concatenate(
@@ -121,25 +122,33 @@
         [along.astype(jnp.bfloat16), turned(along).astype(jnp.bfloat16)], axis=0
     )
     copies[4].wait()
-    modes = dot(first[...], both).astype(jnp.bfloat16)
-    for b in range(KB):
-        for j in range(MX):
-            out[j * KB + b] = modes[j * C : (j + 1) * C, b * 128 : (b + 1) * 128]
-
-
-def prepare_kernel(spectral, out):
+    sent = []
+    for g in range(4):
+        modes = dot(first[g * 4 * C : (g + 1) * 4 * C, :], both).astype(jnp.bfloat16)
+        for b in range(KB):
+            for j in range(4):
+                out[(g * 4 + j) * KB + b] = modes[j * C : (j + 1) * C, b * 128 : (b + 1) * 128]
+        copy = pltpu.make_async_copy(
+            out.at[g * 16 : (g + 1) * 16], out_far.at[g * 16 : (g + 1) * 16], sems.at[5 + g]
+        )
+        copy.start()
+        sent.append(copy)
+    for copy in sent:
+        copy.wait()
+
+
+def prepare_kernel(own, other, out):
     row = lax.broadcasted_iota(jnp.int32, (4 * C, C), 0)
     column = lax.broadcasted_iota(jnp.int32, (4 * C, C), 1)
-    total = jnp.zeros((4 * C, 128), jnp.float32)
-    for d in range(4):
-        piece = jnp.concatenate(
-            [spectral[k, r, d] for r in range(2) for k in range(KL)], axis=0
-        )
-        pick = jnp.where(row == column * 4 + d, 1.0, 0.0).astype(jnp.bfloat16)
-        total = total + dot_nt(pick, piece)
-    weight = total.astype(jnp.bfloat16)
-    for i in range(4):
-        out[i] = weight
+    for n, source in enumerate((own, other)):
+        total = jnp.zeros((4 * C, 128), jnp.float32)
+        for d in range(4):
+            piece = jnp.concatenate(
+                [source[k, r, d] for r in range(2) for k in range(KL)], axis=0
+            )
+            pick = jnp.where(row == column * 4 + d, 1.0, 0.0).astype(jnp.bfloat16)
+            total = total + dot_nt(pick, piece)
+        out[n] = total.astype(jnp.bfloat16)
 
 
 def position_phases():
@@ -160,13 +169,7 @@
     return cosine, sine
 
 
-def collect_kernel(parts, second_far, back_far, out, second, back, cosine, sine, sems):
-    copies = [
-        pltpu.make_async_copy(second_far, second, sems.at[0]),
-        pltpu.make_async_copy(back_far, back, sems.at[1]),
-    ]
-    for copy in copies:
-        copy.start()
+def collect_kernel(parts, out, cosine, sine):
     cosine[...], sine[...] = position_phases()
     real = jnp.zeros((C, 128), jnp.float32)
     imag = jnp.zeros((C, 128), jnp.float32)
@@ -176,11 +179,9 @@
         imag = imag + part * sine[s : s + 1, :]
     total = (real - turned(imag)) * (1.0 / math.sqrt(X * Y * Z))
     out[...] = total
-    for copy in copies:
-        copy.wait()
-
-
-def mix_kernel(total, near, far, cosine, sine, out):
+
+
+def mix_kernel(total, here, before, after, across, cosine, sine, out):
     row = lax.broadcasted_iota(jnp.int32, (4 * C, C), 0)
     column = lax.broadcasted_iota(jnp.int32, (4 * C, C), 1)
     repeat = jnp.where((row >> 2) == column, 1.0, 0.0).astype(jnp.bfloat16)
@@ -199,11 +200,14 @@
         cross = cross + pltpu.roll(cross, 64, 1)
         return jnp.where(lane < 64, same, cross)
 
-    upper = lax.axis_index("col").astype(jnp.int32) & 1
-    nearer = (row >> 2) == upper
-    mixed = jnp.concatenate(
-        [jnp.where(nearer, mixed_with(near[i]), mixed_with(far[i])) for i in range(4)], axis=0
-    )
+    place = lax.axis_index("col").astype(jnp.int32)
+    nearer = (row >> 2) == (place & 1)
+    blocks = [jnp.zeros((8, 128), jnp.float32) for _ in range(4)]
+    for offset, weight in ((0, here), (3, before), (1, after), (2, across)):
+        block = jnp.where(nearer, mixed_with(weight[0]), mixed_with(weight[1]))
+        source = ((place >> 1) + offset) & 3
+        blocks = [jnp.where(source == i, block, blocks[i]) for i in range(4)]
+    mixed = jnp.concatenate(blocks, axis=0)
     mixed_turned = turned(mixed)
     for s in range(64):
         out[s] = (mixed * cosine[s : s + 1, :] + mixed_turned * sine[s : s + 1, :]).astype(
@@ -287,34 +291,33 @@
     first_backward = jnp.asarray(first_backward, bf16)
     anywhere = pl.BlockSpec(memory_space=pl.ANY)
 
+    raw = spectral[0, 0].transpose(0, 1, 3, 4, 2)
+    partner = lax.ppermute(raw, "col", [(i, i ^ 1) for i in range(8)])
     weight = pl.pallas_call(
         prepare_kernel,
-        out_shape=jax.ShapeDtypeStruct((4, 128, 128), bf16),
+        out_shape=jax.ShapeDtypeStruct((2, 128, 128), bf16),
         compiler_params=pltpu.CompilerParams(vmem_limit_bytes=8 << 20),
         name="prepare",
-    )(spectral[0, 0].transpose(0, 1, 3, 4, 2))
-    own = lax.all_to_all(
-        weight,
-        "col",
-        split_axis=0,
-        concat_axis=0,
-        axis_index_groups=[[0, 2, 4, 6], [1, 3, 5, 7]],
-        tiled=True,
-    )
-    other = lax.ppermute(own, "col", [(i, i ^ 1) for i in range(8)])
-
-    modes, hidden, depth = pl.pallas_call(
+    )(raw, partner)
+    around = []
+    for step in (2, 6, 4):
+        around.append(
+            lax.ppermute(weight, "col", [(i, (i + step) % 8) for i in range(8)])
+        )
+
+    modes, hidden = pl.pallas_call(
         forward_kernel,
         in_specs=[anywhere] * 4,
         out_shape=[
-            pltpu.VMEM((64, C, 128), bf16),
+            pltpu.HBM((64, C, 128), bf16),
             pltpu.VMEM(hidden.shape, bf16),
+        ],
+        scratch_shapes=[
             pltpu.VMEM(depth.shape, bf16),
-        ],
-        scratch_shapes=[
             pltpu.VMEM(second.shape, bf16),
             pltpu.VMEM(first_forward.shape, bf16),
-            pltpu.SemaphoreType.DMA((5,)),
+            pltpu.VMEM((64, C, 128), bf16),
+            pltpu.SemaphoreType.DMA((9,)),
         ],
         compiler_params=pltpu.CompilerParams(vmem_limit_bytes=20 << 20),
         name="forward",
@@ -322,27 +325,22 @@
     parts = lax.all_to_all(
         modes, ("gx", "gy"), split_axis=0, concat_axis=0, tiled=True
     )
-    inside = pl.BlockSpec(memory_space=pltpu.VMEM)
-    total, second, first_backward, cosine, sine = pl.pallas_call(
+    total, cosine, sine = pl.pallas_call(
         collect_kernel,
-        in_specs=[inside] + [anywhere] * 2,
         out_shape=[
             pltpu.VMEM((C, 128), jnp.float32),
-            pltpu.VMEM(second.shape, bf16),
-            pltpu.VMEM(first_backward.shape, bf16),
             pltpu.VMEM((64, 128), jnp.float32),
             pltpu.VMEM((64, 128), jnp.float32),
         ],
-        scratch_shapes=[pltpu.SemaphoreType.DMA((2,))],
         compiler_params=pltpu.CompilerParams(vmem_limit_bytes=12 << 20),
         name="collect",
-    )(near(parts), far(second), far(first_backward))
+    )(near(parts))
     mixed = pl.pallas_call(
         mix_kernel,
         out_shape=pltpu.VMEM((64, C, 128), bf16),
         compiler_params=pltpu.CompilerParams(vmem_limit_bytes=12 << 20),
         name="mix",
-    )(total, near(own), near(other), cosine, sine)
+    )(total, near(weight), *[near(w) for w in around], cosine, sine)
     full = lax.all_to_all(mixed, ("gx", "gy"), split_axis=0, concat_axis=0, tiled=True)
     result = pl.pallas_call(
         inverse_kernel,
@@ -359,9 +357,9 @@
     )(
         near(full),
         hidden,
-        depth,
-        second,
-        first_backward,
+        near(depth),
+        near(second),
+        near(first_backward),
         skip_weight,
         skip_bias,
         norm_gain,

time: 76 us -> 75.5 us (level)
  waiting for transfers between devices: 16.5 us -> 5.15 us
  starting transfers between devices: 23.5 us -> 30.7 us
  blocking collectives: 22.5 us -> 25.8 us
  Pallas kernels: 11.3 us -> 13.2 us
  local copies, waits for them, and re-layouts: 1.72 us -> 0.05 us
    ppermute x1 -> x4, starting transfers between devices: 2.05 us -> 15.5 us  [the longest x3 13.6 us: local(): lax.ppermute(weight, 'col', [(i, (i + step) % 8) for i in range(8)])]
    all_to_all x1, waiting for transfers between devices: 12.3 us -> 0.01 us  [local(): lax.all_to_all(modes, ('gx', 'gy'), split_axis=0, concat_axis=0, tiled=True)]
    all_to_all x1 -> x0, starting transfers between devices: 6.19 us -> none  [local(): lax.all_to_all(weight, 'col', split_axis=0, concat_axis=0, axis_index_gro...]
    ppermute x1 -> x4, waiting for transfers between devices: 0.01 us -> 5.15 us  [the longest x3 3.84 us: local(): lax.ppermute(weight, 'col', [(i, (i + step) % 8) for i in range(8)])]
    all_to_all x1 -> x0, waiting for transfers between devices: 4.18 us -> none  [local(): lax.all_to_all(weight, 'col', split_axis=0, concat_axis=0, axis_index_gro...]
    all_to_all x1, blocking collectives: 22.5 us -> 25.8 us  [local(): lax.all_to_all(mixed, ('gx', 'gy'), split_axis=0, concat_axis=0, tiled=True)]
    pallas_call x1, Pallas kernels: 3.83 us -> 6.19 us  [local(): pl.pallas_call(forward_kernel, in_specs=[anywhere] * 4, out_shape=[pltpu....]
    unnamed x12 -> x16, local copies, waits for them, and re-layouts: 1.72 us -> 0.05 us
  transfers between devices with their start and end apart: 3 -> 5, of which waited for: 2 -> 2; matrix products, arithmetic and copies ran while one was open for 0% -> 0% of each run, Pallas kernels for 7% -> 2%
where the time goes in v3:
time: 75.5 us; the launch traced here: 75.1 us
  starting transfers between devices  30.7 us (41%)
  blocking collectives  25.8 us (34%)
  Pallas kernels  13.2 us (17%)
  waiting for transfers between devices  5.15 us (7%)
    all_to_all x1, blocking collectives, local(): lax.all_to_all(mixed, ('gx', 'gy'), split_axis=0, concat_axis=0, tiled=True)  25.8 us
    all_to_all x1, starting transfers between devices, local(): lax.all_to_all(modes, ('gx', 'gy'), split_axis=0, concat_axis=0, tiled=True)  15.2 us
    ppermute x3, starting transfers between devices, local(): lax.ppermute(weight, 'col', [(i, (i + step) % 8) for i in range(8)])  13.6 us
    pallas_call x1, Pallas kernels, local(): pl.pallas_call(forward_kernel, in_specs=[anywhere] * 4, out_shape=[pltpu....  6.19 us
    pallas_call x1, Pallas kernels, local(): pl.pallas_call(inverse_kernel, out_shape=jax.ShapeDtypeStruct((TX, YH, YL...  4.76 us
    ppermute x3, waiting for transfers between devices, local(): lax.ppermute(weight, 'col', [(i, (i + step) % 8) for i in range(8)])  3.84 us
    ppermute x1, starting transfers between devices, local(): partner = lax.ppermute(raw, 'col', [(i, i ^ 1) for i in range(8)])  1.92 us
  transfers between devices with their start and end apart: 5, of which 2 were waited for; matrix products, arithmetic and copies ran while one was open for 0% of the time, Pallas kernels for 2%

profile of v3, /device:TPU:8, one launch (start us, length us, event | category | flops | bytes accessed | tf_op | source)
XLA Modules:
  0.0 75.1 jit_solution(5392045861951638033)
XLA Ops:
  0.0 6.2 %forward.1 = (bf16[64,32,128]{2,1,0:T(8,128)(2,1)}, bf16[8,4,8,32,128]{4,3,2,1,0:T(8,128)(2,1)S(1)}) custom-call(bf16[8,4,8,32,128]{4,3,2,1,0:T(8,128)(2,1)} %bitcast.7, bf16[1024,256]{1,0:T(8,128)(2,1)} %constant.8.clone.depth_far.depth, bf16[1024,512]{1,0:T(8,128)(2,1)} %constant.9.clone.second_far.second, bf16[512,512]{1,0:T(8,128)(2,1)} %constant.10.clone.first_far), custom_call_target="tpu_custom_call" | custom-call | tf_op jit(solution)/shard_map/forward/pallas_call | solution.py:308
  6.2 0.0 copy-start
  6.2 0.0 copy-start.4
  6.2 0.0 copy-start.5
  6.2 0.0 copy-start.6
  6.2 0.0 copy-start.7
  6.3 15.2 %all-to-all-start = ((bf16[64,32,128]{2,1,0:T(8,128)(2,1)}), bf16[64,32,128]{2,1,0:T(8,128)(2,1)}, u32[]{:S(2)}, u32[]{:S(2)}) async-start(bf16[64,32,128]{2,1,0:T(8,128)(2,1)} %get-tuple-element.10), calls=%async_computation | async-start | bytes 1048576 | tf_op jit(solution)/shard_map/all_to_all | solution.py:325
  21.5 1.9 %collective-permute-start = (bf16[4,2,4,16,32]{4,3,2,1,0:T(8,128)(2,1)S(1)}, bf16[4,2,4,16,32]{4,3,2,1,0:T(8,128)(2,1)S(1)}, u32[]{:S(2)}, u32[]{:S(2)}) collective-permute-start(bf16[4,2,4,16,32]{4,3,2,1,0:T(8,128)(2,1)S(1)} %bitcast.5), channel_id=1, source_target_pairs={{0,1},{1,0},{2,3},{3,2},{4,5},{5,4},{6,7},{7,6},{8,9},{9,8},{10,11... | collective-permute-start | bytes 98312 | tf_op jit(solution)/shard_map/ppermute | solution.py:295
  23.4 1.3 %collective-permute-done.other = bf16[4,2,4,16,32]{4,3,2,1,0:T(8,128)(2,1)S(1)} collective-permute-done((bf16[4,2,4,16,32]{4,3,2,1,0:T(8,128)(2,1)S(1)}, bf16[4,2,4,16,32]{4,3,2,1,0:T(8,128)(2,1)S(1)}, u32[]{:S(2)}, u32[]{:S(2)}) %collective-permute-start) | collective-permute-done | bytes 32800 | tf_op jit(solution)/shard_map/ppermute | solution.py:295
  24.7 0.3 prepare.1.here
  25.0 6.8 %collective-permute-start.3 = (bf16[2,128,128]{2,1,0:T(8,128)(2,1)S(1)}, bf16[2,128,128]{2,1,0:T(8,128)(2,1)S(1)}, u32[]{:S(2)}, u32[]{:S(2)}) collective-permute-start(bf16[2,128,128]{2,1,0:T(8,128)(2,1)S(1)} %prepare.1.here), channel_id=1, source_target_pairs={{0,4},{1,5},{2,6},{3,7},{4,0},{5,1},{6,2},{7,3},{8,12},{9,13},{10,... | collective-permute-start | bytes 196616 | tf_op jit(solution)/shard_map/ppermute | solution.py:305
  31.9 3.1 %collective-permute-start.2 = (bf16[2,128,128]{2,1,0:T(8,128)(2,1)S(1)}, bf16[2,128,128]{2,1,0:T(8,128)(2,1)S(1)}, u32[]{:S(2)}, u32[]{:S(2)}) collective-permute-start(bf16[2,128,128]{2,1,0:T(8,128)(2,1)S(1)} %prepare.1.here), channel_id=1, source_target_pairs={{0,6},{1,7},{2,0},{3,1},{4,2},{5,3},{6,4},{7,5},{8,14},{9,15},{10,... | collective-permute-start | bytes 196616 | tf_op jit(solution)/shard_map/ppermute | solution.py:305
  35.0 3.6 %collective-permute-start.1 = (bf16[2,128,128]{2,1,0:T(8,128)(2,1)S(1)}, bf16[2,128,128]{2,1,0:T(8,128)(2,1)S(1)}, u32[]{:S(2)}, u32[]{:S(2)}) collective-permute-start(bf16[2,128,128]{2,1,0:T(8,128)(2,1)S(1)} %prepare.1.here), channel_id=1, source_target_pairs={{0,2},{1,3},{2,4},{3,5},{4,6},{5,7},{6,0},{7,1},{8,10},{9,11},{10,... | collective-permute-start | bytes 196616 | tf_op jit(solution)/shard_map/ppermute | solution.py:305
  38.7 0.0 all-to-all-done.parts
  38.7 0.0 copy-start.1
  38.7 0.0 copy-start.2
  38.7 1.5 %collect.1 = (f32[32,128]{1,0:T(8,128)S(1)}, f32[64,128]{1,0:T(8,128)S(1)}, f32[64,128]{1,0:T(8,128)S(1)}) custom-call(bf16[64,32,128]{2,1,0:T(8,128)(2,1)} %all-to-all-done.parts), custom_call_target="tpu_custom_call" | custom-call | tf_op jit(solution)/shard_map/collect/pallas_call | solution.py:328
  40.2 0.0 collective-permute-done.3.across
  40.2 0.0 collective-permute-done.2.after
  40.2 3.8 %collective-permute-done.1.before = bf16[2,128,128]{2,1,0:T(8,128)(2,1)S(1)} collective-permute-done((bf16[2,128,128]{2,1,0:T(8,128)(2,1)S(1)}, bf16[2,128,128]{2,1,0:T(8,128)(2,1)S(1)}, u32[]{:S(2)}, u32[]{:S(2)}) %collective-permute-start.1) | collective-permute-done | bytes 65568 | tf_op jit(solution)/shard_map/ppermute | solution.py:305
  44.0 0.5 mix.1
  44.5 25.8 %all_to_all.10.modes = bf16[64,32,128]{2,1,0:T(8,128)(2,1)S(1)} all-to-all(bf16[64,32,128]{2,1,0:T(8,128)(2,1)S(1)} %mix.1), channel_id=1, replica_groups=mesh['gx'=16,'gy'=4,'col'=8] {'gx','gy'}, dimensions={0} | all-to-all | bytes 1048576 | tf_op jit(solution)/shard_map/all_to_all | solution.py:344
  70.3 0.0 copy-done
  70.4 4.8 %inverse.1 = bf16[8,4,8,32,128]{4,3,2,1,0:T(8,128)(2,1)} custom-call(bf16[64,32,128]{2,1,0:T(8,128)(2,1)S(1)} %all_to_all.10.modes, bf16[8,4,8,32,128]{4,3,2,1,0:T(8,128)(2,1)S(1)} %get-tuple-element.14.fields, bf16[1024,256]{1,0:T(8,128)(2,1)S(1)} %copy-done.1, bf16[1024,512]{1,0:T(8,128)(2,1)S(1)} %copy-done, bf16[512,512]{1,0:T(8,128)(2,1)S(1)} %copy-done.2, ...), custom_call_target="tpu_custom_call" | custom-call | tf_op jit(solution)/shard_map/inverse/pallas_call | solution.py:345
  (8 shorter events, 0.0 us)
Async XLA Ops:
  0.0 21.5 %copy-start.3 = (bf16[1,1,4,2,32,4,16]{4,6,5,3,2,1,0:T(8,128)(2,1)S(1)}, bf16[1,1,4,2,32,4,16]{4,6,5,3,2,1,0:T(8,128)(2,1)}, u32[]{:S(2)}) copy-start(bf16[1,1,4,2,32,4,16]{4,6,5,3,2,1,0:T(8,128)(2,1)} %param.11) | copy-start | bytes 98308
  6.2 64.1 %copy-start = (bf16[1024,512]{1,0:T(8,128)(2,1)S(1)}, bf16[1024,512]{1,0:T(8,128)(2,1)}, u32[]{:S(2)}) copy-start(bf16[1024,512]{1,0:T(8,128)(2,1)} %constant.9.clone.second_far.second) | copy-start | bytes 3145732
  6.2 64.1 %copy-start.4 = (bf16[1,32,32]{2,1,0:T(8,128)(2,1)S(1)}, bf16[1,32,32]{2,1,0:T(8,128)(2,1)}, u32[]{:S(2)}) copy-start(bf16[1,32,32]{2,1,0:T(8,128)(2,1)} %skip.1) | copy-start | bytes 6148
  6.2 64.1 %copy-start.5 = (f32[1,32]{1,0:T(1,128)S(1)}, f32[1,32]{1,0:T(1,128)}, u32[]{:S(2)}) copy-start(f32[1,32]{1,0:T(1,128)} %bias.1) | copy-start | bytes 388
  6.2 64.1 %copy-start.6 = (f32[1,32]{1,0:T(1,128)S(1)}, f32[1,32]{1,0:T(1,128)}, u32[]{:S(2)}) copy-start(f32[1,32]{1,0:T(1,128)} %gain.1) | copy-start | bytes 388
  6.2 64.1 %copy-start.7 = (f32[1,32]{1,0:T(1,128)S(1)}, f32[1,32]{1,0:T(1,128)}, u32[]{:S(2)}) copy-start(f32[1,32]{1,0:T(1,128)} %shift.1) | copy-start | bytes 388
  6.3 32.4 %all-to-all-start = ((bf16[64,32,128]{2,1,0:T(8,128)(2,1)}), bf16[64,32,128]{2,1,0:T(8,128)(2,1)}, u32[]{:S(2)}, u32[]{:S(2)}) async-start(bf16[64,32,128]{2,1,0:T(8,128)(2,1)} %get-tuple-element.10), calls=%async_computation | async-start | bytes 1048576 | tf_op jit(solution)/shard_map/all_to_all | solution.py:325
  21.5 3.2 %collective-permute-start = (bf16[4,2,4,16,32]{4,3,2,1,0:T(8,128)(2,1)S(1)}, bf16[4,2,4,16,32]{4,3,2,1,0:T(8,128)(2,1)S(1)}, u32[]{:S(2)}, u32[]{:S(2)}) collective-permute-start(bf16[4,2,4,16,32]{4,3,2,1,0:T(8,128)(2,1)S(1)} %bitcast.5), channel_id=1, source_target_pairs={{0,1},{1,0},{2,3},{3,2},{4,5},{5,4},{6,7},{7,6},{8,9},{9,8},{10,11... | collective-permute-start | bytes 98312 | tf_op jit(solution)/shard_map/ppermute | solution.py:295
  25.0 15.1 %collective-permute-start.3 = (bf16[2,128,128]{2,1,0:T(8,128)(2,1)S(1)}, bf16[2,128,128]{2,1,0:T(8,128)(2,1)S(1)}, u32[]{:S(2)}, u32[]{:S(2)}) collective-permute-start(bf16[2,128,128]{2,1,0:T(8,128)(2,1)S(1)} %prepare.1.here), channel_id=1, source_target_pairs={{0,4},{1,5},{2,6},{3,7},{4,0},{5,1},{6,2},{7,3},{8,12},{9,13},{10,... | collective-permute-start | bytes 196616 | tf_op jit(solution)/shard_map/ppermute | solution.py:305
  31.9 8.3 %collective-permute-start.2 = (bf16[2,128,128]{2,1,0:T(8,128)(2,1)S(1)}, bf16[2,128,128]{2,1,0:T(8,128)(2,1)S(1)}, u32[]{:S(2)}, u32[]{:S(2)}) collective-permute-start(bf16[2,128,128]{2,1,0:T(8,128)(2,1)S(1)} %prepare.1.here), channel_id=1, source_target_pairs={{0,6},{1,7},{2,0},{3,1},{4,2},{5,3},{6,4},{7,5},{8,14},{9,15},{10,... | collective-permute-start | bytes 196616 | tf_op jit(solution)/shard_map/ppermute | solution.py:305
  35.0 9.0 %collective-permute-start.1 = (bf16[2,128,128]{2,1,0:T(8,128)(2,1)S(1)}, bf16[2,128,128]{2,1,0:T(8,128)(2,1)S(1)}, u32[]{:S(2)}, u32[]{:S(2)}) collective-permute-start(bf16[2,128,128]{2,1,0:T(8,128)(2,1)S(1)} %prepare.1.here), channel_id=1, source_target_pairs={{0,2},{1,3},{2,4},{3,5},{4,6},{5,7},{6,0},{7,1},{8,10},{9,11},{10,... | collective-permute-start | bytes 196616 | tf_op jit(solution)/shard_map/ppermute | solution.py:305
  38.7 31.7 %copy-start.1 = (bf16[1024,256]{1,0:T(8,128)(2,1)S(1)}, bf16[1024,256]{1,0:T(8,128)(2,1)}, u32[]{:S(2)}) copy-start(bf16[1024,256]{1,0:T(8,128)(2,1)} %constant.8.clone.depth_far.depth) | copy-start | bytes 1572868
  38.7 31.7 %copy-start.2 = (bf16[512,512]{1,0:T(8,128)(2,1)S(1)}, bf16[512,512]{1,0:T(8,128)(2,1)}, u32[]{:S(2)}) copy-start(bf16[512,512]{1,0:T(8,128)(2,1)} %constant.11.clone.first) | copy-start | bytes 1572868

commit v4 on v3

--- a/solution.py
+++ b/solution.py
@@ -93,13 +93,12 @@
     copies = [
         pltpu.make_async_copy(here, there, sems.at[n]) for n, (here, there) in enumerate(pairs)
     ]
-    for copy in copies[:3]:
+    for copy in copies:
         copy.start()
     copies[0].wait()
     amplitudes = []
     for part in range(2):
         copies[1 + part].wait()
-        copies[3 + part].start()
         amplitude = None
         for p in range(YL // 2):
             left = jnp.concatenate(
@@ -169,11 +168,21 @@
     return cosine, sine
 
 
-def collect_kernel(parts, out, cosine, sine):
+def collect_kernel(parts_far, out, cosine, sine, parts, sems):
+    copies = [
+        pltpu.make_async_copy(
+            parts_far.at[g * 16 : (g + 1) * 16], parts.at[g * 16 : (g + 1) * 16], sems.at[g]
+        )
+        for g in range(4)
+    ]
+    for copy in copies:
+        copy.start()
     cosine[...], sine[...] = position_phases()
     real = jnp.zeros((C, 128), jnp.float32)
     imag = jnp.zeros((C, 128), jnp.float32)
     for s in range(64):
+        if s % 16 == 0:
+            copies[s // 16].wait()
         part = parts[s].astype(jnp.float32)
         real = real + part * cosine[s : s + 1, :]
         imag = imag + part * sine[s : s + 1, :]
@@ -234,16 +243,24 @@
     )
     both = dot(first[...], full)
     lines = both[: TX * C] + turned(both[TX * C :])
-    lines = (lines * (1.0 / math.sqrt(MX * MY * MZ))).astype(jnp.bfloat16)
+    lines = lines * (1.0 / math.sqrt(MX * MY * MZ))
+    lines = lines.reshape(TX, C, YH * 128)
+    lines = lines - jnp.sum(lines, axis=1, keepdims=True) * (1.0 / C)
+    lines = lines.reshape(TX * C, YH * 128).astype(jnp.bfloat16)
     rows[...] = dot_nt(lines, second[...]).astype(jnp.bfloat16)
     row = lax.broadcasted_iota(jnp.int32, (YL * C, YL * C), 0)
     column = lax.broadcasted_iota(jnp.int32, (YL * C, YL * C), 1)
-    wide = jnp.concatenate([skip[0]] * YL, axis=1)
-    tall = jnp.concatenate([wide] * YL, axis=0).astype(jnp.float32)
-    skips = jnp.where((row >> 5) == (column >> 5), tall, 0.0).astype(jnp.bfloat16)
+    block = (row >> 5) == (column >> 5)
+    square = skip[0].astype(jnp.float32)
+    square = square - jnp.sum(square, axis=0, keepdims=True) * (1.0 / C)
+    wide = jnp.concatenate([square] * YL, axis=1)
+    tall = jnp.where(block, jnp.concatenate([wide] * YL, axis=0), 0.0)
+    coarse = tall.astype(jnp.bfloat16)
+    fine = (tall - coarse.astype(jnp.float32)).astype(jnp.bfloat16)
     bias = column_of(bias)
-    gain = column_of(gain)
-    shift = column_of(shift)
+    bias = bias - jnp.sum(bias, axis=0, keepdims=True) * (1.0 / C)
+    gain = column_of(gain) * math.sqrt(0.5)
+    shift = column_of(shift) * math.sqrt(0.5)
     copies = []
     for h in range(YH):
         spectral[h % 2] = dot_nt(rows[:, h * 256 : (h + 1) * 256], depth[...])
@@ -251,7 +268,7 @@
             cells = jnp.concatenate(
                 [fields[x + i, h].reshape(YL * C, Z) for i in range(2)], axis=1
             )
-            skipped = dot(skips, cells)
+            skipped = dot(coarse, cells) + dot(fine, cells)
             for i in range(2):
                 for y in range(YL):
                     pre = (
@@ -259,16 +276,15 @@
                         + skipped[y * C : (y + 1) * C, i * Z : (i + 1) * Z]
                         + bias
                     )
-                    centre = jnp.sum(pre, axis=0, keepdims=True) * (1.0 / C)
-                    pre = pre - centre
                     spread = jnp.sum(pre * pre, axis=0, keepdims=True) * (1.0 / C)
                     normed = pre * lax.rsqrt(spread + norm_eps) * gain + shift
-                    half = normed * 0.5
-                    value = half * lax.erf(normed * math.sqrt(0.5)) + half
-                    done[h, x + i, y] = value.astype(jnp.bfloat16)
-        copy = pltpu.make_async_copy(done.at[h], out.at[:, h], sems.at[h])
-        copy.start()
-        copies.append(copy)
+                    half = normed * math.sqrt(0.5)
+                    done[h, x + i, y] = (half * lax.erf(normed) + half).astype(jnp.bfloat16)
+            copy = pltpu.make_async_copy(
+                done.at[h, x : x + 2], out.at[x : x + 2, h], sems.at[h * 4 + x // 2]
+            )
+            copy.start()
+            copies.append(copy)
     for copy in copies:
         copy.wait()
 
@@ -327,6 +343,8 @@
     )
     total, cosine, sine = pl.pallas_call(
         collect_kernel,
+        in_specs=[anywhere],
+        scratch_shapes=[pltpu.VMEM((64, C, 128), bf16), pltpu.SemaphoreType.DMA((4,))],
         out_shape=[
             pltpu.VMEM((C, 128), jnp.float32),
             pltpu.VMEM((64, 128), jnp.float32),
@@ -334,7 +352,7 @@
         ],
         compiler_params=pltpu.CompilerParams(vmem_limit_bytes=12 << 20),
         name="collect",
-    )(near(parts))
+    )(far(parts))
     mixed = pl.pallas_call(
         mix_kernel,
         out_shape=pltpu.VMEM((64, C, 128), bf16),
@@ -350,7 +368,7 @@
             pltpu.VMEM((TX * C, YH * 256), bf16),
             pltpu.VMEM((2, TX * C, YL * Z), jnp.float32),
             pltpu.VMEM((YH, TX, YL, C, Z), bf16),
-            pltpu.SemaphoreType.DMA((YH,)),
+            pltpu.SemaphoreType.DMA((YH * 4,)),
         ],
         compiler_params=pltpu.CompilerParams(vmem_limit_bytes=24 << 20),
         name="inverse",

time: 75.5 us -> 75.2 us (level)
  no operation moved by 1% of the time
where the time goes in v4:
time: 75.2 us; the launch traced here: 74.9 us
  starting transfers between devices  30.7 us (41%)
  blocking collectives  25.8 us (34%)
  Pallas kernels  12.8 us (17%)
  waiting for transfers between devices  5.28 us (7%)
    all_to_all x1, blocking collectives, local(): lax.all_to_all(mixed, ('gx', 'gy'), split_axis=0, concat_axis=0, tiled=True)  25.8 us
    all_to_all x1, starting transfers between devices, local(): lax.all_to_all(modes, ('gx', 'gy'), split_axis=0, concat_axis=0, tiled=True)  15.2 us
    ppermute x3, starting transfers between devices, local(): lax.ppermute(weight, 'col', [(i, (i + step) % 8) for i in range(8)])  13.6 us
    pallas_call x1, Pallas kernels, local(): pl.pallas_call(forward_kernel, in_specs=[anywhere] * 4, out_shape=[pltpu....  5.84 us
    pallas_call x1, Pallas kernels, local(): pl.pallas_call(inverse_kernel, out_shape=jax.ShapeDtypeStruct((TX, YH, YL...  4.84 us
    ppermute x3, waiting for transfers between devices, local(): lax.ppermute(weight, 'col', [(i, (i + step) % 8) for i in range(8)])  3.97 us
    ppermute x1, starting transfers between devices, local(): partner = lax.ppermute(raw, 'col', [(i, i ^ 1) for i in range(8)])  1.92 us
  transfers between devices with their start and end apart: 5, of which 2 were waited for; matrix products, arithmetic and copies ran while one was open for 0% of the time, Pallas kernels for 2%

profile of v4, /device:TPU:8, one launch (start us, length us, event | category | flops | bytes accessed | tf_op | source)
XLA Modules:
  0.0 74.9 jit_solution(14700763058940339249)
XLA Ops:
  0.0 5.8 %forward.1 = (bf16[64,32,128]{2,1,0:T(8,128)(2,1)}, bf16[8,4,8,32,128]{4,3,2,1,0:T(8,128)(2,1)S(1)}) custom-call(bf16[8,4,8,32,128]{4,3,2,1,0:T(8,128)(2,1)} %bitcast.7, bf16[1024,256]{1,0:T(8,128)(2,1)} %constant.8.clone.depth_far.depth, bf16[1024,512]{1,0:T(8,128)(2,1)} %constant.9.clone.second_far.second, bf16[512,512]{1,0:T(8,128)(2,1)} %constant.10.clone.first_far), custom_call_target="tpu_custom_call" | custom-call | tf_op jit(solution)/shard_map/forward/pallas_call | solution.py:324
  5.8 0.0 copy-start
  5.9 0.0 copy-start.4
  5.9 0.0 copy-start.5
  5.9 0.0 copy-start.6
  5.9 0.0 copy-start.7
  5.9 15.2 %all-to-all-start = ((bf16[64,32,128]{2,1,0:T(8,128)(2,1)}), bf16[64,32,128]{2,1,0:T(8,128)(2,1)}, u32[]{:S(2)}, u32[]{:S(2)}) async-start(bf16[64,32,128]{2,1,0:T(8,128)(2,1)} %get-tuple-element.10), calls=%async_computation | async-start | bytes 1048576 | tf_op jit(solution)/shard_map/all_to_all | solution.py:341
  21.2 1.9 %collective-permute-start = (bf16[4,2,4,16,32]{4,3,2,1,0:T(8,128)(2,1)S(1)}, bf16[4,2,4,16,32]{4,3,2,1,0:T(8,128)(2,1)S(1)}, u32[]{:S(2)}, u32[]{:S(2)}) collective-permute-start(bf16[4,2,4,16,32]{4,3,2,1,0:T(8,128)(2,1)S(1)} %bitcast.5), channel_id=1, source_target_pairs={{0,1},{1,0},{2,3},{3,2},{4,5},{5,4},{6,7},{7,6},{8,9},{9,8},{10,11... | collective-permute-start | bytes 98312 | tf_op jit(solution)/shard_map/ppermute | solution.py:311
  23.1 1.3 %collective-permute-done.other = bf16[4,2,4,16,32]{4,3,2,1,0:T(8,128)(2,1)S(1)} collective-permute-done((bf16[4,2,4,16,32]{4,3,2,1,0:T(8,128)(2,1)S(1)}, bf16[4,2,4,16,32]{4,3,2,1,0:T(8,128)(2,1)S(1)}, u32[]{:S(2)}, u32[]{:S(2)}) %collective-permute-start) | collective-permute-done | bytes 32800 | tf_op jit(solution)/shard_map/ppermute | solution.py:311
  24.4 0.3 prepare.1.here
  24.7 6.8 %collective-permute-start.3 = (bf16[2,128,128]{2,1,0:T(8,128)(2,1)S(1)}, bf16[2,128,128]{2,1,0:T(8,128)(2,1)S(1)}, u32[]{:S(2)}, u32[]{:S(2)}) collective-permute-start(bf16[2,128,128]{2,1,0:T(8,128)(2,1)S(1)} %prepare.1.here), channel_id=1, source_target_pairs={{0,4},{1,5},{2,6},{3,7},{4,0},{5,1},{6,2},{7,3},{8,12},{9,13},{10,... | collective-permute-start | bytes 196616 | tf_op jit(solution)/shard_map/ppermute | solution.py:321
  31.5 3.1 %collective-permute-start.2 = (bf16[2,128,128]{2,1,0:T(8,128)(2,1)S(1)}, bf16[2,128,128]{2,1,0:T(8,128)(2,1)S(1)}, u32[]{:S(2)}, u32[]{:S(2)}) collective-permute-start(bf16[2,128,128]{2,1,0:T(8,128)(2,1)S(1)} %prepare.1.here), channel_id=1, source_target_pairs={{0,6},{1,7},{2,0},{3,1},{4,2},{5,3},{6,4},{7,5},{8,14},{9,15},{10,... | collective-permute-start | bytes 196616 | tf_op jit(solution)/shard_map/ppermute | solution.py:321
  34.7 3.6 %collective-permute-start.1 = (bf16[2,128,128]{2,1,0:T(8,128)(2,1)S(1)}, bf16[2,128,128]{2,1,0:T(8,128)(2,1)S(1)}, u32[]{:S(2)}, u32[]{:S(2)}) collective-permute-start(bf16[2,128,128]{2,1,0:T(8,128)(2,1)S(1)} %prepare.1.here), channel_id=1, source_target_pairs={{0,2},{1,3},{2,4},{3,5},{4,6},{5,7},{6,0},{7,1},{8,10},{9,11},{10,... | collective-permute-start | bytes 196616 | tf_op jit(solution)/shard_map/ppermute | solution.py:321
  38.3 0.0 all-to-all-done.parts_far
  38.3 0.0 copy-start.1
  38.3 0.0 copy-start.2
  38.3 1.3 %collect.1 = (f32[32,128]{1,0:T(8,128)S(1)}, f32[64,128]{1,0:T(8,128)S(1)}, f32[64,128]{1,0:T(8,128)S(1)}) custom-call(bf16[64,32,128]{2,1,0:T(8,128)(2,1)} %all-to-all-done.parts_far), custom_call_target="tpu_custom_call" | custom-call | tf_op jit(solution)/shard_map/collect/pallas_call | solution.py:344
  39.7 0.0 collective-permute-done.3.across
  39.7 0.0 collective-permute-done.2.after
  39.7 4.0 %collective-permute-done.1.before = bf16[2,128,128]{2,1,0:T(8,128)(2,1)S(1)} collective-permute-done((bf16[2,128,128]{2,1,0:T(8,128)(2,1)S(1)}, bf16[2,128,128]{2,1,0:T(8,128)(2,1)S(1)}, u32[]{:S(2)}, u32[]{:S(2)}) %collective-permute-start.1) | collective-permute-done | bytes 65568 | tf_op jit(solution)/shard_map/ppermute | solution.py:321
  43.7 0.5 mix.1
  44.2 25.8 %all_to_all.10.modes = bf16[64,32,128]{2,1,0:T(8,128)(2,1)S(1)} all-to-all(bf16[64,32,128]{2,1,0:T(8,128)(2,1)S(1)} %mix.1), channel_id=1, replica_groups=mesh['gx'=16,'gy'=4,'col'=8] {'gx','gy'}, dimensions={0} | all-to-all | bytes 1048576 | tf_op jit(solution)/shard_map/all_to_all | solution.py:362
  70.0 0.0 copy-done
  70.0 4.8 %inverse.1 = bf16[8,4,8,32,128]{4,3,2,1,0:T(8,128)(2,1)} custom-call(bf16[64,32,128]{2,1,0:T(8,128)(2,1)S(1)} %all_to_all.10.modes, bf16[8,4,8,32,128]{4,3,2,1,0:T(8,128)(2,1)S(1)} %get-tuple-element.14.fields, bf16[1024,256]{1,0:T(8,128)(2,1)S(1)} %copy-done.1, bf16[1024,512]{1,0:T(8,128)(2,1)S(1)} %copy-done, bf16[512,512]{1,0:T(8,128)(2,1)S(1)} %copy-done.2, ...), custom_call_target="tpu_custom_call" | custom-call | tf_op jit(solution)/shard_map/inverse/pallas_call | solution.py:363
  (8 shorter events, 0.0 us)
Async XLA Ops:
  0.0 21.1 %copy-start.3 = (bf16[1,1,4,2,32,4,16]{4,6,5,3,2,1,0:T(8,128)(2,1)S(1)}, bf16[1,1,4,2,32,4,16]{4,6,5,3,2,1,0:T(8,128)(2,1)}, u32[]{:S(2)}) copy-start(bf16[1,1,4,2,32,4,16]{4,6,5,3,2,1,0:T(8,128)(2,1)} %param.11) | copy-start | bytes 98308
  5.8 64.1 %copy-start = (bf16[1024,512]{1,0:T(8,128)(2,1)S(1)}, bf16[1024,512]{1,0:T(8,128)(2,1)}, u32[]{:S(2)}) copy-start(bf16[1024,512]{1,0:T(8,128)(2,1)} %constant.9.clone.second_far.second) | copy-start | bytes 3145732
  5.9 64.1 %copy-start.4 = (bf16[1,32,32]{2,1,0:T(8,128)(2,1)S(1)}, bf16[1,32,32]{2,1,0:T(8,128)(2,1)}, u32[]{:S(2)}) copy-start(bf16[1,32,32]{2,1,0:T(8,128)(2,1)} %skip.1) | copy-start | bytes 6148
  5.9 64.1 %copy-start.5 = (f32[1,32]{1,0:T(1,128)S(1)}, f32[1,32]{1,0:T(1,128)}, u32[]{:S(2)}) copy-start(f32[1,32]{1,0:T(1,128)} %bias.1) | copy-start | bytes 388
  5.9 64.1 %copy-start.6 = (f32[1,32]{1,0:T(1,128)S(1)}, f32[1,32]{1,0:T(1,128)}, u32[]{:S(2)}) copy-start(f32[1,32]{1,0:T(1,128)} %gain.1) | copy-start | bytes 388
  5.9 64.1 %copy-start.7 = (f32[1,32]{1,0:T(1,128)S(1)}, f32[1,32]{1,0:T(1,128)}, u32[]{:S(2)}) copy-start(f32[1,32]{1,0:T(1,128)} %shift.1) | copy-start | bytes 388
  5.9 32.4 %all-to-all-start = ((bf16[64,32,128]{2,1,0:T(8,128)(2,1)}), bf16[64,32,128]{2,1,0:T(8,128)(2,1)}, u32[]{:S(2)}, u32[]{:S(2)}) async-start(bf16[64,32,128]{2,1,0:T(8,128)(2,1)} %get-tuple-element.10), calls=%async_computation | async-start | bytes 1048576 | tf_op jit(solution)/shard_map/all_to_all | solution.py:341
  21.2 3.2 %collective-permute-start = (bf16[4,2,4,16,32]{4,3,2,1,0:T(8,128)(2,1)S(1)}, bf16[4,2,4,16,32]{4,3,2,1,0:T(8,128)(2,1)S(1)}, u32[]{:S(2)}, u32[]{:S(2)}) collective-permute-start(bf16[4,2,4,16,32]{4,3,2,1,0:T(8,128)(2,1)S(1)} %bitcast.5), channel_id=1, source_target_pairs={{0,1},{1,0},{2,3},{3,2},{4,5},{5,4},{6,7},{7,6},{8,9},{9,8},{10,11... | collective-permute-start | bytes 98312 | tf_op jit(solution)/shard_map/ppermute | solution.py:311
  24.7 15.0 %collective-permute-start.3 = (bf16[2,128,128]{2,1,0:T(8,128)(2,1)S(1)}, bf16[2,128,128]{2,1,0:T(8,128)(2,1)S(1)}, u32[]{:S(2)}, u32[]{:S(2)}) collective-permute-start(bf16[2,128,128]{2,1,0:T(8,128)(2,1)S(1)} %prepare.1.here), channel_id=1, source_target_pairs={{0,4},{1,5},{2,6},{3,7},{4,0},{5,1},{6,2},{7,3},{8,12},{9,13},{10,... | collective-permute-start | bytes 196616 | tf_op jit(solution)/shard_map/ppermute | solution.py:321
  31.5 8.1 %collective-permute-start.2 = (bf16[2,128,128]{2,1,0:T(8,128)(2,1)S(1)}, bf16[2,128,128]{2,1,0:T(8,128)(2,1)S(1)}, u32[]{:S(2)}, u32[]{:S(2)}) collective-permute-start(bf16[2,128,128]{2,1,0:T(8,128)(2,1)S(1)} %prepare.1.here), channel_id=1, source_target_pairs={{0,6},{1,7},{2,0},{3,1},{4,2},{5,3},{6,4},{7,5},{8,14},{9,15},{10,... | collective-permute-start | bytes 196616 | tf_op jit(solution)/shard_map/ppermute | solution.py:321
  34.7 9.0 %collective-permute-start.1 = (bf16[2,128,128]{2,1,0:T(8,128)(2,1)S(1)}, bf16[2,128,128]{2,1,0:T(8,128)(2,1)S(1)}, u32[]{:S(2)}, u32[]{:S(2)}) collective-permute-start(bf16[2,128,128]{2,1,0:T(8,128)(2,1)S(1)} %prepare.1.here), channel_id=1, source_target_pairs={{0,2},{1,3},{2,4},{3,5},{4,6},{5,7},{6,0},{7,1},{8,10},{9,11},{10,... | collective-permute-start | bytes 196616 | tf_op jit(solution)/shard_map/ppermute | solution.py:321
  38.3 31.7 %copy-start.1 = (bf16[1024,256]{1,0:T(8,128)(2,1)S(1)}, bf16[1024,256]{1,0:T(8,128)(2,1)}, u32[]{:S(2)}) copy-start(bf16[1024,256]{1,0:T(8,128)(2,1)} %constant.8.clone.depth_far.depth) | copy-start | bytes 1572868
  38.3 31.7 %copy-start.2 = (bf16[512,512]{1,0:T(8,128)(2,1)S(1)}, bf16[512,512]{1,0:T(8,128)(2,1)}, u32[]{:S(2)}) copy-start(bf16[512,512]{1,0:T(8,128)(2,1)} %constant.11.clone.first) | copy-start | bytes 1572868

commit v5 on v4

--- a/solution.py
+++ b/solution.py
@@ -80,7 +80,7 @@
 
 
 def forward_kernel(
-    fields_far, depth_far, second_far, first_far, out_far, fields, depth, second, first, out, sems
+    fields_far, depth_far, second_far, first_far, out, fields, depth, second, first, sems
 ):
     half = TX // 2
     pairs = [
@@ -93,8 +93,8 @@
     copies = [
         pltpu.make_async_copy(here, there, sems.at[n]) for n, (here, there) in enumerate(pairs)
     ]
-    for copy in copies:
-        copy.start()
+    for n, copy in enumerate(copies):
+        copy.start(priority=0 if n < 3 else 1)
     copies[0].wait()
     amplitudes = []
     for part in range(2):
@@ -121,19 +121,10 @@
         [along.astype(jnp.bfloat16), turned(along).astype(jnp.bfloat16)], axis=0
     )
     copies[4].wait()
-    sent = []
-    for g in range(4):
-        modes = dot(first[g * 4 * C : (g + 1) * 4 * C, :], both).astype(jnp.bfloat16)
+    modes = dot(first[...], both).astype(jnp.bfloat16)
+    for j in range(MX):
         for b in range(KB):
-            for j in range(4):
-                out[(g * 4 + j) * KB + b] = modes[j * C : (j + 1) * C, b * 128 : (b + 1) * 128]
-        copy = pltpu.make_async_copy(
-            out.at[g * 16 : (g + 1) * 16], out_far.at[g * 16 : (g + 1) * 16], sems.at[5 + g]
-        )
-        copy.start()
-        sent.append(copy)
-    for copy in sent:
-        copy.wait()
+            out[j * KB + b] = modes[j * C : (j + 1) * C, b * 128 : (b + 1) * 128]
 
 
 def prepare_kernel(own, other, out):
@@ -255,8 +246,7 @@
     square = square - jnp.sum(square, axis=0, keepdims=True) * (1.0 / C)
     wide = jnp.concatenate([square] * YL, axis=1)
     tall = jnp.where(block, jnp.concatenate([wide] * YL, axis=0), 0.0)
-    coarse = tall.astype(jnp.bfloat16)
-    fine = (tall - coarse.astype(jnp.float32)).astype(jnp.bfloat16)
+    skips = tall.astype(jnp.bfloat16)
     bias = column_of(bias)
     bias = bias - jnp.sum(bias, axis=0, keepdims=True) * (1.0 / C)
     gain = column_of(gain) * math.sqrt(0.5)
@@ -268,7 +258,7 @@
             cells = jnp.concatenate(
                 [fields[x + i, h].reshape(YL * C, Z) for i in range(2)], axis=1
             )
-            skipped = dot(coarse, cells) + dot(fine, cells)
+            skipped = dot(skips, cells)
             for i in range(2):
                 for y in range(YL):
                     pre = (
@@ -316,24 +306,24 @@
         name="prepare",
     )(raw, partner)
     around = []
-    for step in (2, 6, 4):
+    for step in (4, 2, 6):
+        source = weight
         around.append(
-            lax.ppermute(weight, "col", [(i, (i + step) % 8) for i in range(8)])
+            lax.ppermute(source, "col", [(i, (i + step) % 8) for i in range(8)])
         )
 
     modes, hidden = pl.pallas_call(
         forward_kernel,
         in_specs=[anywhere] * 4,
         out_shape=[
-            pltpu.HBM((64, C, 128), bf16),
+            pltpu.VMEM((64, C, 128), bf16),
             pltpu.VMEM(hidden.shape, bf16),
         ],
         scratch_shapes=[
             pltpu.VMEM(depth.shape, bf16),
             pltpu.VMEM(second.shape, bf16),
             pltpu.VMEM(first_forward.shape, bf16),
-            pltpu.VMEM((64, C, 128), bf16),
-            pltpu.SemaphoreType.DMA((9,)),
+            pltpu.SemaphoreType.DMA((5,)),
         ],
         compiler_params=pltpu.CompilerParams(vmem_limit_bytes=20 << 20),
         name="forward",
@@ -358,7 +348,7 @@
         out_shape=pltpu.VMEM((64, C, 128), bf16),
         compiler_params=pltpu.CompilerParams(vmem_limit_bytes=12 << 20),
         name="mix",
-    )(total, near(weight), *[near(w) for w in around], cosine, sine)
+    )(total, near(weight), *[near(around[n]) for n in (1, 2, 0)], cosine, sine)
     full = lax.all_to_all(mixed, ("gx", "gy"), split_axis=0, concat_axis=0, tiled=True)
     result = pl.pallas_call(
         inverse_kernel,

time: 75.2 us -> 73.7 us (0.980)
  Pallas kernels: 12.8 us -> 10.5 us
  local copies, waits for them, and re-layouts: 0.05 us -> 0.83 us
    pallas_call x1, Pallas kernels: 5.84 us -> 3.86 us  [local(): pl.pallas_call(forward_kernel, in_specs=[anywhere] * 4, out_shape=[pltpu....]
    unnamed x16 -> x18, local copies, waits for them, and re-layouts: 0.05 us -> 0.83 us
where the time goes in v5:
time: 73.7 us; the launch traced here: 73.3 us
  starting transfers between devices  30.7 us (42%)
  blocking collectives  25.8 us (35%)
  Pallas kernels  10.5 us (14%)
  waiting for transfers between devices  5.29 us (7%)
  local copies, waits for them, and re-layouts  0.83 us (1%)
    all_to_all x1, blocking collectives, local(): lax.all_to_all(mixed, ('gx', 'gy'), split_axis=0, concat_axis=0, tiled=True)  25.8 us
    all_to_all x1, starting transfers between devices, local(): lax.all_to_all(modes, ('gx', 'gy'), split_axis=0, concat_axis=0, tiled=True)  15.2 us
    ppermute x3, starting transfers between devices, local(): lax.ppermute(source, 'col', [(i, (i + step) % 8) for i in range(8)])  13.6 us
    pallas_call x1, Pallas kernels, local(): pl.pallas_call(inverse_kernel, out_shape=jax.ShapeDtypeStruct((TX, YH, YL...  4.53 us
    ppermute x3, waiting for transfers between devices, local(): lax.ppermute(source, 'col', [(i, (i + step) % 8) for i in range(8)])  3.97 us
    pallas_call x1, Pallas kernels, local(): pl.pallas_call(forward_kernel, in_specs=[anywhere] * 4, out_shape=[pltpu....  3.86 us
    ppermute x1, starting transfers between devices, local(): partner = lax.ppermute(raw, 'col', [(i, i ^ 1) for i in range(8)])  1.92 us
  transfers between devices with their start and end apart: 5, of which 2 were waited for; matrix products, arithmetic and copies ran while one was open for 0% of the time, Pallas kernels for 2%

profile of v5, /device:TPU:8, one launch (start us, length us, event | category | flops | bytes accessed | tf_op | source)
XLA Modules:
  0.0 73.3 jit_solution(15078607869999243112)
XLA Ops:
  0.0 3.9 %forward.1 = (bf16[64,32,128]{2,1,0:T(8,128)(2,1)S(1)}, bf16[8,4,8,32,128]{4,3,2,1,0:T(8,128)(2,1)S(1)}) custom-call(bf16[8,4,8,32,128]{4,3,2,1,0:T(8,128)(2,1)} %bitcast.7, bf16[1024,256]{1,0:T(8,128)(2,1)} %constant.8.clone.depth_far.depth, bf16[1024,512]{1,0:T(8,128)(2,1)} %constant.9.clone.second_far.second, bf16[512,512]{1,0:T(8,128)(2,1)} %constant.10.clone.first_far), custom_call_target="tpu_custom_call" | custom-call | tf_op jit(solution)/shard_map/forward/pallas_call | solution.py:315
  3.9 0.0 copy-start.3
  3.9 0.8 %copy-done.3 = bf16[64,32,128]{2,1,0:T(8,128)(2,1)} copy-done((bf16[64,32,128]{2,1,0:T(8,128)(2,1)}, bf16[64,32,128]{2,1,0:T(8,128)(2,1)S(1)}, u32[]{:S(2)}) %copy-start.3) | copy-done | bytes 524312
  4.7 0.0 copy-start.8
  4.7 15.2 %all-to-all-start = ((bf16[64,32,128]{2,1,0:T(8,128)(2,1)}), bf16[64,32,128]{2,1,0:T(8,128)(2,1)}, u32[]{:S(2)}, u32[]{:S(2)}) async-start(bf16[64,32,128]{2,1,0:T(8,128)(2,1)} %copy-done.3), calls=%async_computation | async-start | bytes 1048576 | tf_op jit(solution)/shard_map/all_to_all | solution.py:331
  19.9 0.0 copy-done.4
  19.9 1.9 %collective-permute-start = (bf16[4,2,4,16,32]{4,3,2,1,0:T(8,128)(2,1)S(1)}, bf16[4,2,4,16,32]{4,3,2,1,0:T(8,128)(2,1)S(1)}, u32[]{:S(2)}, u32[]{:S(2)}) collective-permute-start(bf16[4,2,4,16,32]{4,3,2,1,0:T(8,128)(2,1)S(1)} %bitcast.5), channel_id=1, source_target_pairs={{0,1},{1,0},{2,3},{3,2},{4,5},{5,4},{6,7},{7,6},{8,9},{9,8},{10,11... | collective-permute-start | bytes 98312 | tf_op jit(solution)/shard_map/ppermute | solution.py:301
  21.9 1.3 %collective-permute-done.other = bf16[4,2,4,16,32]{4,3,2,1,0:T(8,128)(2,1)S(1)} collective-permute-done((bf16[4,2,4,16,32]{4,3,2,1,0:T(8,128)(2,1)S(1)}, bf16[4,2,4,16,32]{4,3,2,1,0:T(8,128)(2,1)S(1)}, u32[]{:S(2)}, u32[]{:S(2)}) %collective-permute-start) | collective-permute-done | bytes 32800 | tf_op jit(solution)/shard_map/ppermute | solution.py:301
  23.2 0.3 prepare.1.here
  23.5 6.8 %collective-permute-start.3 = (bf16[2,128,128]{2,1,0:T(8,128)(2,1)S(1)}, bf16[2,128,128]{2,1,0:T(8,128)(2,1)S(1)}, u32[]{:S(2)}, u32[]{:S(2)}) collective-permute-start(bf16[2,128,128]{2,1,0:T(8,128)(2,1)S(1)} %prepare.1.here), channel_id=1, source_target_pairs={{0,4},{1,5},{2,6},{3,7},{4,0},{5,1},{6,2},{7,3},{8,12},{9,13},{10,... | collective-permute-start | bytes 196616 | tf_op jit(solution)/shard_map/ppermute | solution.py:312
  30.3 3.1 %collective-permute-start.2 = (bf16[2,128,128]{2,1,0:T(8,128)(2,1)S(1)}, bf16[2,128,128]{2,1,0:T(8,128)(2,1)S(1)}, u32[]{:S(2)}, u32[]{:S(2)}) collective-permute-start(bf16[2,128,128]{2,1,0:T(8,128)(2,1)S(1)} %prepare.1.here), channel_id=1, source_target_pairs={{0,6},{1,7},{2,0},{3,1},{4,2},{5,3},{6,4},{7,5},{8,14},{9,15},{10,... | collective-permute-start | bytes 196616 | tf_op jit(solution)/shard_map/ppermute | solution.py:312
  33.5 3.6 %collective-permute-start.1 = (bf16[2,128,128]{2,1,0:T(8,128)(2,1)S(1)}, bf16[2,128,128]{2,1,0:T(8,128)(2,1)S(1)}, u32[]{:S(2)}, u32[]{:S(2)}) collective-permute-start(bf16[2,128,128]{2,1,0:T(8,128)(2,1)S(1)} %prepare.1.here), channel_id=1, source_target_pairs={{0,2},{1,3},{2,4},{3,5},{4,6},{5,7},{6,0},{7,1},{8,10},{9,11},{10,... | collective-permute-start | bytes 196616 | tf_op jit(solution)/shard_map/ppermute | solution.py:312
  37.1 0.0 all-to-all-done.parts_far
  37.1 0.0 copy-start.1
  37.1 0.0 copy-start.2
  37.1 1.3 %collect.1 = (f32[32,128]{1,0:T(8,128)S(1)}, f32[64,128]{1,0:T(8,128)S(1)}, f32[64,128]{1,0:T(8,128)S(1)}) custom-call(bf16[64,32,128]{2,1,0:T(8,128)(2,1)} %all-to-all-done.parts_far), custom_call_target="tpu_custom_call" | custom-call | tf_op jit(solution)/shard_map/collect/pallas_call | solution.py:334
  38.4 0.0 collective-permute-done.3.across
  38.5 0.0 collective-permute-done.2.after
  38.5 4.0 %collective-permute-done.1.before = bf16[2,128,128]{2,1,0:T(8,128)(2,1)S(1)} collective-permute-done((bf16[2,128,128]{2,1,0:T(8,128)(2,1)S(1)}, bf16[2,128,128]{2,1,0:T(8,128)(2,1)S(1)}, u32[]{:S(2)}, u32[]{:S(2)}) %collective-permute-start.1) | collective-permute-done | bytes 65568 | tf_op jit(solution)/shard_map/ppermute | solution.py:312
  42.4 0.5 mix.1
  42.9 25.8 %all_to_all.10.modes = bf16[64,32,128]{2,1,0:T(8,128)(2,1)S(1)} all-to-all(bf16[64,32,128]{2,1,0:T(8,128)(2,1)S(1)} %mix.1), channel_id=1, replica_groups=mesh['gx'=16,'gy'=4,'col'=8] {'gx','gy'}, dimensions={0} | all-to-all | bytes 1048576 | tf_op jit(solution)/shard_map/all_to_all | solution.py:352
  68.7 0.0 copy-done
  68.7 0.0 copy-done.5
  68.8 4.5 %inverse.1 = bf16[8,4,8,32,128]{4,3,2,1,0:T(8,128)(2,1)} custom-call(bf16[64,32,128]{2,1,0:T(8,128)(2,1)S(1)} %all_to_all.10.modes, bf16[8,4,8,32,128]{4,3,2,1,0:T(8,128)(2,1)S(1)} %get-tuple-element.14.fields, bf16[1024,256]{1,0:T(8,128)(2,1)S(1)} %copy-done.1, bf16[1024,512]{1,0:T(8,128)(2,1)S(1)} %copy-done, bf16[512,512]{1,0:T(8,128)(2,1)S(1)} %copy-done.2, ...), custom_call_target="tpu_custom_call" | custom-call | tf_op jit(solution)/shard_map/inverse/pallas_call | solution.py:353
  (10 shorter events, 0.0 us)
Async XLA Ops:
  0.0 19.9 %copy-start.4 = (bf16[1,1,4,2,32,4,16]{4,6,5,3,2,1,0:T(8,128)(2,1)S(1)}, bf16[1,1,4,2,32,4,16]{4,6,5,3,2,1,0:T(8,128)(2,1)}, u32[]{:S(2)}) copy-start(bf16[1,1,4,2,32,4,16]{4,6,5,3,2,1,0:T(8,128)(2,1)} %param.11) | copy-start | bytes 98308
  3.9 0.8 %copy-start.3 = (bf16[64,32,128]{2,1,0:T(8,128)(2,1)}, bf16[64,32,128]{2,1,0:T(8,128)(2,1)S(1)}, u32[]{:S(2)}) copy-start(bf16[64,32,128]{2,1,0:T(8,128)(2,1)S(1)} %get-tuple-element.10) | copy-start | bytes 1572868
  4.7 64.1 %copy-start = (bf16[1024,512]{1,0:T(8,128)(2,1)S(1)}, bf16[1024,512]{1,0:T(8,128)(2,1)}, u32[]{:S(2)}) copy-start(bf16[1024,512]{1,0:T(8,128)(2,1)} %constant.9.clone.second_far.second) | copy-start | bytes 3145732
  4.7 64.1 %copy-start.5 = (bf16[1,32,32]{2,1,0:T(8,128)(2,1)S(1)}, bf16[1,32,32]{2,1,0:T(8,128)(2,1)}, u32[]{:S(2)}) copy-start(bf16[1,32,32]{2,1,0:T(8,128)(2,1)} %skip.1) | copy-start | bytes 6148
  4.7 64.1 %copy-start.6 = (f32[1,32]{1,0:T(1,128)S(1)}, f32[1,32]{1,0:T(1,128)}, u32[]{:S(2)}) copy-start(f32[1,32]{1,0:T(1,128)} %bias.1) | copy-start | bytes 388
  4.7 64.1 %copy-start.7 = (f32[1,32]{1,0:T(1,128)S(1)}, f32[1,32]{1,0:T(1,128)}, u32[]{:S(2)}) copy-start(f32[1,32]{1,0:T(1,128)} %gain.1) | copy-start | bytes 388
  4.7 64.1 %copy-start.8 = (f32[1,32]{1,0:T(1,128)S(1)}, f32[1,32]{1,0:T(1,128)}, u32[]{:S(2)}) copy-start(f32[1,32]{1,0:T(1,128)} %shift.1) | copy-start | bytes 388
  4.7 32.4 %all-to-all-start = ((bf16[64,32,128]{2,1,0:T(8,128)(2,1)}), bf16[64,32,128]{2,1,0:T(8,128)(2,1)}, u32[]{:S(2)}, u32[]{:S(2)}) async-start(bf16[64,32,128]{2,1,0:T(8,128)(2,1)} %copy-done.3), calls=%async_computation | async-start | bytes 1048576 | tf_op jit(solution)/shard_map/all_to_all | solution.py:331
  19.9 3.2 %collective-permute-start = (bf16[4,2,4,16,32]{4,3,2,1,0:T(8,128)(2,1)S(1)}, bf16[4,2,4,16,32]{4,3,2,1,0:T(8,128)(2,1)S(1)}, u32[]{:S(2)}, u32[]{:S(2)}) collective-permute-start(bf16[4,2,4,16,32]{4,3,2,1,0:T(8,128)(2,1)S(1)} %bitcast.5), channel_id=1, source_target_pairs={{0,1},{1,0},{2,3},{3,2},{4,5},{5,4},{6,7},{7,6},{8,9},{9,8},{10,11... | collective-permute-start | bytes 98312 | tf_op jit(solution)/shard_map/ppermute | solution.py:301
  23.5 15.0 %collective-permute-start.3 = (bf16[2,128,128]{2,1,0:T(8,128)(2,1)S(1)}, bf16[2,128,128]{2,1,0:T(8,128)(2,1)S(1)}, u32[]{:S(2)}, u32[]{:S(2)}) collective-permute-start(bf16[2,128,128]{2,1,0:T(8,128)(2,1)S(1)} %prepare.1.here), channel_id=1, source_target_pairs={{0,4},{1,5},{2,6},{3,7},{4,0},{5,1},{6,2},{7,3},{8,12},{9,13},{10,... | collective-permute-start | bytes 196616 | tf_op jit(solution)/shard_map/ppermute | solution.py:312
  30.3 8.1 %collective-permute-start.2 = (bf16[2,128,128]{2,1,0:T(8,128)(2,1)S(1)}, bf16[2,128,128]{2,1,0:T(8,128)(2,1)S(1)}, u32[]{:S(2)}, u32[]{:S(2)}) collective-permute-start(bf16[2,128,128]{2,1,0:T(8,128)(2,1)S(1)} %prepare.1.here), channel_id=1, source_target_pairs={{0,6},{1,7},{2,0},{3,1},{4,2},{5,3},{6,4},{7,5},{8,14},{9,15},{10,... | collective-permute-start | bytes 196616 | tf_op jit(solution)/shard_map/ppermute | solution.py:312
  33.5 9.0 %collective-permute-start.1 = (bf16[2,128,128]{2,1,0:T(8,128)(2,1)S(1)}, bf16[2,128,128]{2,1,0:T(8,128)(2,1)S(1)}, u32[]{:S(2)}, u32[]{:S(2)}) collective-permute-start(bf16[2,128,128]{2,1,0:T(8,128)(2,1)S(1)} %prepare.1.here), channel_id=1, source_target_pairs={{0,2},{1,3},{2,4},{3,5},{4,6},{5,7},{6,0},{7,1},{8,10},{9,11},{10,... | collective-permute-start | bytes 196616 | tf_op jit(solution)/shard_map/ppermute | solution.py:312
  37.1 31.7 %copy-start.1 = (bf16[1024,256]{1,0:T(8,128)(2,1)S(1)}, bf16[1024,256]{1,0:T(8,128)(2,1)}, u32[]{:S(2)}) copy-start(bf16[1024,256]{1,0:T(8,128)(2,1)} %constant.8.clone.depth_far.depth) | copy-start | bytes 1572868
  37.1 31.7 %copy-start.2 = (bf16[512,512]{1,0:T(8,128)(2,1)S(1)}, bf16[512,512]{1,0:T(8,128)(2,1)}, u32[]{:S(2)}) copy-start(bf16[512,512]{1,0:T(8,128)(2,1)} %constant.11.clone.first) | copy-start | bytes 1572868

commit v6 on v5

--- a/solution.py
+++ b/solution.py
@@ -215,15 +215,16 @@
         )
 
 
-def column_of(vector):
+def column_of(vector, scale=1.0):
     row = lax.broadcasted_iota(jnp.int32, (C, C), 0)
     column = lax.broadcasted_iota(jnp.int32, (C, C), 1)
-    spread = jnp.where(row == column, jnp.broadcast_to(vector[...], (C, C)), 0.0)
+    spread = jnp.where(row == column, jnp.broadcast_to(vector[...] * scale, (C, C)), 0.0)
     return jnp.broadcast_to(jnp.sum(spread, axis=1, keepdims=True), (C, Z))
 
 
 def inverse_kernel(
-    modes, fields, depth, second, first, skip, bias, gain, shift, out, rows, spectral, done, sems
+    modes, fields, depth, second, first, skip, bias_row, gain_row, shift_row,
+    out, bias, gain, shift, spectral, done, sems,
 ):
     full = jnp.concatenate(
         [
@@ -238,7 +239,6 @@
     lines = lines.reshape(TX, C, YH * 128)
     lines = lines - jnp.sum(lines, axis=1, keepdims=True) * (1.0 / C)
     lines = lines.reshape(TX * C, YH * 128).astype(jnp.bfloat16)
-    rows[...] = dot_nt(lines, second[...]).astype(jnp.bfloat16)
     row = lax.broadcasted_iota(jnp.int32, (YL * C, YL * C), 0)
     column = lax.broadcasted_iota(jnp.int32, (YL * C, YL * C), 1)
     block = (row >> 5) == (column >> 5)
@@ -247,13 +247,14 @@
     wide = jnp.concatenate([square] * YL, axis=1)
     tall = jnp.where(block, jnp.concatenate([wide] * YL, axis=0), 0.0)
     skips = tall.astype(jnp.bfloat16)
-    bias = column_of(bias)
-    bias = bias - jnp.sum(bias, axis=0, keepdims=True) * (1.0 / C)
-    gain = column_of(gain) * math.sqrt(0.5)
-    shift = column_of(shift) * math.sqrt(0.5)
+    offset = column_of(bias_row)
+    bias[...] = offset - jnp.sum(offset, axis=0, keepdims=True) * (1.0 / C)
+    gain[...] = column_of(gain_row, math.sqrt(0.5 * C))
+    shift[...] = column_of(shift_row, math.sqrt(0.5))
     copies = []
     for h in range(YH):
-        spectral[h % 2] = dot_nt(rows[:, h * 256 : (h + 1) * 256], depth[...])
+        rows = dot_nt(lines, second[h * 256 : (h + 1) * 256, :]).astype(jnp.bfloat16)
+        spectral[h % 2] = dot_nt(rows, depth[...])
         for x in range(0, TX, 2):
             cells = jnp.concatenate(
                 [fields[x + i, h].reshape(YL * C, Z) for i in range(2)], axis=1
@@ -264,10 +265,10 @@
                     pre = (
                         spectral[h % 2, (x + i) * C : (x + i + 1) * C, y * Z : (y + 1) * Z]
                         + skipped[y * C : (y + 1) * C, i * Z : (i + 1) * Z]
-                        + bias
+                        + bias[...]
                     )
-                    spread = jnp.sum(pre * pre, axis=0, keepdims=True) * (1.0 / C)
-                    normed = pre * lax.rsqrt(spread + norm_eps) * gain + shift
+                    spread = jnp.sum(pre * pre, axis=0, keepdims=True)
+                    normed = pre * lax.rsqrt(spread + C * norm_eps) * gain[...] + shift[...]
                     half = normed * math.sqrt(0.5)
                     done[h, x + i, y] = (half * lax.erf(normed) + half).astype(jnp.bfloat16)
             copy = pltpu.make_async_copy(
@@ -355,7 +356,9 @@
         out_shape=jax.ShapeDtypeStruct((TX, YH, YL, C, Z), bf16),
         out_specs=anywhere,
         scratch_shapes=[
-            pltpu.VMEM((TX * C, YH * 256), bf16),
+            pltpu.VMEM((C, Z), jnp.float32),
+            pltpu.VMEM((C, Z), jnp.float32),
+            pltpu.VMEM((C, Z), jnp.float32),
             pltpu.VMEM((2, TX * C, YL * Z), jnp.float32),
             pltpu.VMEM((YH, TX, YL, C, Z), bf16),
             pltpu.SemaphoreType.DMA((YH * 4,)),

time: 73.7 us -> 73.2 us (level)
  no operation moved by 1% of the time
where the time goes in v6:
time: 73.2 us; the launch traced here: 72.9 us
  starting transfers between devices  30.7 us (42%)
  blocking collectives  25.8 us (35%)
  Pallas kernels  10.1 us (14%)
  waiting for transfers between devices  5.29 us (7%)
  local copies, waits for them, and re-layouts  0.83 us (1%)
    all_to_all x1, blocking collectives, local(): lax.all_to_all(mixed, ('gx', 'gy'), split_axis=0, concat_axis=0, tiled=True)  25.8 us
    all_to_all x1, starting transfers between devices, local(): lax.all_to_all(modes, ('gx', 'gy'), split_axis=0, concat_axis=0, tiled=True)  15.2 us
    ppermute x3, starting transfers between devices, local(): lax.ppermute(source, 'col', [(i, (i + step) % 8) for i in range(8)])  13.6 us
    pallas_call x1, Pallas kernels, local(): pl.pallas_call(inverse_kernel, out_shape=jax.ShapeDtypeStruct((TX, YH, YL...  4.12 us
    ppermute x3, waiting for transfers between devices, local(): lax.ppermute(source, 'col', [(i, (i + step) % 8) for i in range(8)])  3.97 us
    pallas_call x1, Pallas kernels, local(): pl.pallas_call(forward_kernel, in_specs=[anywhere] * 4, out_shape=[pltpu....  3.86 us
    ppermute x1, starting transfers between devices, local(): partner = lax.ppermute(raw, 'col', [(i, i ^ 1) for i in range(8)])  1.92 us
  transfers between devices with their start and end apart: 5, of which 2 were waited for; matrix products, arithmetic and copies ran while one was open for 0% of the time, Pallas kernels for 2%

profile of v6, /device:TPU:8, one launch (start us, length us, event | category | flops | bytes accessed | tf_op | source)
XLA Modules:
  0.0 72.9 jit_solution(9838773626807837392)
XLA Ops:
  0.0 3.9 %forward.1 = (bf16[64,32,128]{2,1,0:T(8,128)(2,1)S(1)}, bf16[8,4,8,32,128]{4,3,2,1,0:T(8,128)(2,1)S(1)}) custom-call(bf16[8,4,8,32,128]{4,3,2,1,0:T(8,128)(2,1)} %bitcast.7, bf16[1024,256]{1,0:T(8,128)(2,1)} %constant.8.clone.depth_far.depth, bf16[1024,512]{1,0:T(8,128)(2,1)} %constant.9.clone.second_far.second, bf16[512,512]{1,0:T(8,128)(2,1)} %constant.10.clone.first_far), custom_call_target="tpu_custom_call" | custom-call | tf_op jit(solution)/shard_map/forward/pallas_call | solution.py:316
  3.9 0.0 copy-start.3
  3.9 0.8 %copy-done.3 = bf16[64,32,128]{2,1,0:T(8,128)(2,1)} copy-done((bf16[64,32,128]{2,1,0:T(8,128)(2,1)}, bf16[64,32,128]{2,1,0:T(8,128)(2,1)S(1)}, u32[]{:S(2)}) %copy-start.3) | copy-done | bytes 524312
  4.7 0.0 copy-start.8
  4.7 15.2 %all-to-all-start = ((bf16[64,32,128]{2,1,0:T(8,128)(2,1)}), bf16[64,32,128]{2,1,0:T(8,128)(2,1)}, u32[]{:S(2)}, u32[]{:S(2)}) async-start(bf16[64,32,128]{2,1,0:T(8,128)(2,1)} %copy-done.3), calls=%async_computation | async-start | bytes 1048576 | tf_op jit(solution)/shard_map/all_to_all | solution.py:332
  19.9 0.0 copy-done.4
  19.9 1.9 %collective-permute-start = (bf16[4,2,4,16,32]{4,3,2,1,0:T(8,128)(2,1)S(1)}, bf16[4,2,4,16,32]{4,3,2,1,0:T(8,128)(2,1)S(1)}, u32[]{:S(2)}, u32[]{:S(2)}) collective-permute-start(bf16[4,2,4,16,32]{4,3,2,1,0:T(8,128)(2,1)S(1)} %bitcast.5), channel_id=1, source_target_pairs={{0,1},{1,0},{2,3},{3,2},{4,5},{5,4},{6,7},{7,6},{8,9},{9,8},{10,11... | collective-permute-start | bytes 98312 | tf_op jit(solution)/shard_map/ppermute | solution.py:302
  21.9 1.3 %collective-permute-done.other = bf16[4,2,4,16,32]{4,3,2,1,0:T(8,128)(2,1)S(1)} collective-permute-done((bf16[4,2,4,16,32]{4,3,2,1,0:T(8,128)(2,1)S(1)}, bf16[4,2,4,16,32]{4,3,2,1,0:T(8,128)(2,1)S(1)}, u32[]{:S(2)}, u32[]{:S(2)}) %collective-permute-start) | collective-permute-done | bytes 32800 | tf_op jit(solution)/shard_map/ppermute | solution.py:302
  23.2 0.3 prepare.1.here
  23.5 6.8 %collective-permute-start.3 = (bf16[2,128,128]{2,1,0:T(8,128)(2,1)S(1)}, bf16[2,128,128]{2,1,0:T(8,128)(2,1)S(1)}, u32[]{:S(2)}, u32[]{:S(2)}) collective-permute-start(bf16[2,128,128]{2,1,0:T(8,128)(2,1)S(1)} %prepare.1.here), channel_id=1, source_target_pairs={{0,4},{1,5},{2,6},{3,7},{4,0},{5,1},{6,2},{7,3},{8,12},{9,13},{10,... | collective-permute-start | bytes 196616 | tf_op jit(solution)/shard_map/ppermute | solution.py:313
  30.3 3.1 %collective-permute-start.2 = (bf16[2,128,128]{2,1,0:T(8,128)(2,1)S(1)}, bf16[2,128,128]{2,1,0:T(8,128)(2,1)S(1)}, u32[]{:S(2)}, u32[]{:S(2)}) collective-permute-start(bf16[2,128,128]{2,1,0:T(8,128)(2,1)S(1)} %prepare.1.here), channel_id=1, source_target_pairs={{0,6},{1,7},{2,0},{3,1},{4,2},{5,3},{6,4},{7,5},{8,14},{9,15},{10,... | collective-permute-start | bytes 196616 | tf_op jit(solution)/shard_map/ppermute | solution.py:313
  33.5 3.6 %collective-permute-start.1 = (bf16[2,128,128]{2,1,0:T(8,128)(2,1)S(1)}, bf16[2,128,128]{2,1,0:T(8,128)(2,1)S(1)}, u32[]{:S(2)}, u32[]{:S(2)}) collective-permute-start(bf16[2,128,128]{2,1,0:T(8,128)(2,1)S(1)} %prepare.1.here), channel_id=1, source_target_pairs={{0,2},{1,3},{2,4},{3,5},{4,6},{5,7},{6,0},{7,1},{8,10},{9,11},{10,... | collective-permute-start | bytes 196616 | tf_op jit(solution)/shard_map/ppermute | solution.py:313
  37.1 0.0 all-to-all-done.parts_far
  37.1 0.0 copy-start.1
  37.1 0.0 copy-start.2
  37.1 1.3 %collect.1 = (f32[32,128]{1,0:T(8,128)S(1)}, f32[64,128]{1,0:T(8,128)S(1)}, f32[64,128]{1,0:T(8,128)S(1)}) custom-call(bf16[64,32,128]{2,1,0:T(8,128)(2,1)} %all-to-all-done.parts_far), custom_call_target="tpu_custom_call" | custom-call | tf_op jit(solution)/shard_map/collect/pallas_call | solution.py:335
  38.4 0.0 collective-permute-done.3.across
  38.5 0.0 collective-permute-done.2.after
  38.5 4.0 %collective-permute-done.1.before = bf16[2,128,128]{2,1,0:T(8,128)(2,1)S(1)} collective-permute-done((bf16[2,128,128]{2,1,0:T(8,128)(2,1)S(1)}, bf16[2,128,128]{2,1,0:T(8,128)(2,1)S(1)}, u32[]{:S(2)}, u32[]{:S(2)}) %collective-permute-start.1) | collective-permute-done | bytes 65568 | tf_op jit(solution)/shard_map/ppermute | solution.py:313
  42.4 0.5 mix.1
  42.9 25.8 %all_to_all.10.modes = bf16[64,32,128]{2,1,0:T(8,128)(2,1)S(1)} all-to-all(bf16[64,32,128]{2,1,0:T(8,128)(2,1)S(1)} %mix.1), channel_id=1, replica_groups=mesh['gx'=16,'gy'=4,'col'=8] {'gx','gy'}, dimensions={0} | all-to-all | bytes 1048576 | tf_op jit(solution)/shard_map/all_to_all | solution.py:353
  68.7 0.0 copy-done
  68.7 0.0 copy-done.5
  68.8 4.1 %inverse.1 = bf16[8,4,8,32,128]{4,3,2,1,0:T(8,128)(2,1)} custom-call(bf16[64,32,128]{2,1,0:T(8,128)(2,1)S(1)} %all_to_all.10.modes, bf16[8,4,8,32,128]{4,3,2,1,0:T(8,128)(2,1)S(1)} %get-tuple-element.14.fields, bf16[1024,256]{1,0:T(8,128)(2,1)S(1)} %copy-done.1, bf16[1024,512]{1,0:T(8,128)(2,1)S(1)} %copy-done, bf16[512,512]{1,0:T(8,128)(2,1)S(1)} %copy-done.2, ...), custom_call_target="tpu_custom_call" | custom-call | tf_op jit(solution)/shard_map/inverse/pallas_call | solution.py:354
  (10 shorter events, 0.0 us)
Async XLA Ops:
  0.0 19.9 %copy-start.4 = (bf16[1,1,4,2,32,4,16]{4,6,5,3,2,1,0:T(8,128)(2,1)S(1)}, bf16[1,1,4,2,32,4,16]{4,6,5,3,2,1,0:T(8,128)(2,1)}, u32[]{:S(2)}) copy-start(bf16[1,1,4,2,32,4,16]{4,6,5,3,2,1,0:T(8,128)(2,1)} %param.11) | copy-start | bytes 98308
  3.9 0.8 %copy-start.3 = (bf16[64,32,128]{2,1,0:T(8,128)(2,1)}, bf16[64,32,128]{2,1,0:T(8,128)(2,1)S(1)}, u32[]{:S(2)}) copy-start(bf16[64,32,128]{2,1,0:T(8,128)(2,1)S(1)} %get-tuple-element.10) | copy-start | bytes 1572868
  4.7 64.1 %copy-start = (bf16[1024,512]{1,0:T(8,128)(2,1)S(1)}, bf16[1024,512]{1,0:T(8,128)(2,1)}, u32[]{:S(2)}) copy-start(bf16[1024,512]{1,0:T(8,128)(2,1)} %constant.9.clone.second_far.second) | copy-start | bytes 3145732
  4.7 64.1 %copy-start.5 = (bf16[1,32,32]{2,1,0:T(8,128)(2,1)S(1)}, bf16[1,32,32]{2,1,0:T(8,128)(2,1)}, u32[]{:S(2)}) copy-start(bf16[1,32,32]{2,1,0:T(8,128)(2,1)} %skip.1) | copy-start | bytes 6148
  4.7 64.1 %copy-start.6 = (f32[1,32]{1,0:T(1,128)S(1)}, f32[1,32]{1,0:T(1,128)}, u32[]{:S(2)}) copy-start(f32[1,32]{1,0:T(1,128)} %bias_row.1) | copy-start | bytes 388
  4.7 64.1 %copy-start.7 = (f32[1,32]{1,0:T(1,128)S(1)}, f32[1,32]{1,0:T(1,128)}, u32[]{:S(2)}) copy-start(f32[1,32]{1,0:T(1,128)} %gain_row.1) | copy-start | bytes 388
  4.7 64.1 %copy-start.8 = (f32[1,32]{1,0:T(1,128)S(1)}, f32[1,32]{1,0:T(1,128)}, u32[]{:S(2)}) copy-start(f32[1,32]{1,0:T(1,128)} %shift_row.1) | copy-start | bytes 388
  4.7 32.4 %all-to-all-start = ((bf16[64,32,128]{2,1,0:T(8,128)(2,1)}), bf16[64,32,128]{2,1,0:T(8,128)(2,1)}, u32[]{:S(2)}, u32[]{:S(2)}) async-start(bf16[64,32,128]{2,1,0:T(8,128)(2,1)} %copy-done.3), calls=%async_computation | async-start | bytes 1048576 | tf_op jit(solution)/shard_map/all_to_all | solution.py:332
  19.9 3.2 %collective-permute-start = (bf16[4,2,4,16,32]{4,3,2,1,0:T(8,128)(2,1)S(1)}, bf16[4,2,4,16,32]{4,3,2,1,0:T(8,128)(2,1)S(1)}, u32[]{:S(2)}, u32[]{:S(2)}) collective-permute-start(bf16[4,2,4,16,32]{4,3,2,1,0:T(8,128)(2,1)S(1)} %bitcast.5), channel_id=1, source_target_pairs={{0,1},{1,0},{2,3},{3,2},{4,5},{5,4},{6,7},{7,6},{8,9},{9,8},{10,11... | collective-permute-start | bytes 98312 | tf_op jit(solution)/shard_map/ppermute | solution.py:302
  23.5 15.0 %collective-permute-start.3 = (bf16[2,128,128]{2,1,0:T(8,128)(2,1)S(1)}, bf16[2,128,128]{2,1,0:T(8,128)(2,1)S(1)}, u32[]{:S(2)}, u32[]{:S(2)}) collective-permute-start(bf16[2,128,128]{2,1,0:T(8,128)(2,1)S(1)} %prepare.1.here), channel_id=1, source_target_pairs={{0,4},{1,5},{2,6},{3,7},{4,0},{5,1},{6,2},{7,3},{8,12},{9,13},{10,... | collective-permute-start | bytes 196616 | tf_op jit(solution)/shard_map/ppermute | solution.py:313
  30.3 8.1 %collective-permute-start.2 = (bf16[2,128,128]{2,1,0:T(8,128)(2,1)S(1)}, bf16[2,128,128]{2,1,0:T(8,128)(2,1)S(1)}, u32[]{:S(2)}, u32[]{:S(2)}) collective-permute-start(bf16[2,128,128]{2,1,0:T(8,128)(2,1)S(1)} %prepare.1.here), channel_id=1, source_target_pairs={{0,6},{1,7},{2,0},{3,1},{4,2},{5,3},{6,4},{7,5},{8,14},{9,15},{10,... | collective-permute-start | bytes 196616 | tf_op jit(solution)/shard_map/ppermute | solution.py:313
  33.5 9.0 %collective-permute-start.1 = (bf16[2,128,128]{2,1,0:T(8,128)(2,1)S(1)}, bf16[2,128,128]{2,1,0:T(8,128)(2,1)S(1)}, u32[]{:S(2)}, u32[]{:S(2)}) collective-permute-start(bf16[2,128,128]{2,1,0:T(8,128)(2,1)S(1)} %prepare.1.here), channel_id=1, source_target_pairs={{0,2},{1,3},{2,4},{3,5},{4,6},{5,7},{6,0},{7,1},{8,10},{9,11},{10,... | collective-permute-start | bytes 196616 | tf_op jit(solution)/shard_map/ppermute | solution.py:313
  37.1 31.7 %copy-start.1 = (bf16[1024,256]{1,0:T(8,128)(2,1)S(1)}, bf16[1024,256]{1,0:T(8,128)(2,1)}, u32[]{:S(2)}) copy-start(bf16[1024,256]{1,0:T(8,128)(2,1)} %constant.8.clone.depth_far.depth) | copy-start | bytes 1572868
  37.1 31.7 %copy-start.2 = (bf16[512,512]{1,0:T(8,128)(2,1)S(1)}, bf16[512,512]{1,0:T(8,128)(2,1)}, u32[]{:S(2)}) copy-start(bf16[512,512]{1,0:T(8,128)(2,1)} %constant.11.clone.first) | copy-start | bytes 1572868

commit v7 on v6

--- a/solution.py
+++ b/solution.py
@@ -162,9 +162,9 @@
 def collect_kernel(parts_far, out, cosine, sine, parts, sems):
     copies = [
         pltpu.make_async_copy(
-            parts_far.at[g * 16 : (g + 1) * 16], parts.at[g * 16 : (g + 1) * 16], sems.at[g]
+            parts_far.at[g * 8 : (g + 1) * 8], parts.at[g * 8 : (g + 1) * 8], sems.at[g]
         )
-        for g in range(4)
+        for g in range(8)
     ]
     for copy in copies:
         copy.start()
@@ -172,8 +172,8 @@
     real = jnp.zeros((C, 128), jnp.float32)
     imag = jnp.zeros((C, 128), jnp.float32)
     for s in range(64):
-        if s % 16 == 0:
-            copies[s // 16].wait()
+        if s % 8 == 0:
+            copies[s // 8].wait()
         part = parts[s].astype(jnp.float32)
         real = real + part * cosine[s : s + 1, :]
         imag = imag + part * sine[s : s + 1, :]
@@ -271,11 +271,11 @@
                     normed = pre * lax.rsqrt(spread + C * norm_eps) * gain[...] + shift[...]
                     half = normed * math.sqrt(0.5)
                     done[h, x + i, y] = (half * lax.erf(normed) + half).astype(jnp.bfloat16)
-            copy = pltpu.make_async_copy(
-                done.at[h, x : x + 2], out.at[x : x + 2, h], sems.at[h * 4 + x // 2]
-            )
-            copy.start()
-            copies.append(copy)
+                copy = pltpu.make_async_copy(
+                    done.at[h, x + i], out.at[x + i, h], sems.at[h * TX + x + i]
+                )
+                copy.start()
+                copies.append(copy)
     for copy in copies:
         copy.wait()
 
@@ -335,7 +335,7 @@
     total, cosine, sine = pl.pallas_call(
         collect_kernel,
         in_specs=[anywhere],
-        scratch_shapes=[pltpu.VMEM((64, C, 128), bf16), pltpu.SemaphoreType.DMA((4,))],
+        scratch_shapes=[pltpu.VMEM((64, C, 128), bf16), pltpu.SemaphoreType.DMA((8,))],
         out_shape=[
             pltpu.VMEM((C, 128), jnp.float32),
             pltpu.VMEM((64, 128), jnp.float32),
@@ -361,7 +361,7 @@
             pltpu.VMEM((C, Z), jnp.float32),
             pltpu.VMEM((2, TX * C, YL * Z), jnp.float32),
             pltpu.VMEM((YH, TX, YL, C, Z), bf16),
-            pltpu.SemaphoreType.DMA((YH * 4,)),
+            pltpu.SemaphoreType.DMA((YH * TX,)),
         ],
         compiler_params=pltpu.CompilerParams(vmem_limit_bytes=24 << 20),
         name="inverse",

time: 73.2 us -> 73.4 us (level)
  no operation moved by 1% of the time
where the time goes in v7:
time: 73.4 us; the launch traced here: 73.1 us
  starting transfers between devices  30.7 us (42%)
  blocking collectives  25.8 us (35%)
  Pallas kernels  10.3 us (14%)
  waiting for transfers between devices  5.31 us (7%)
  local copies, waits for them, and re-layouts  0.83 us (1%)
    all_to_all x1, blocking collectives, local(): lax.all_to_all(mixed, ('gx', 'gy'), split_axis=0, concat_axis=0, tiled=True)  25.8 us
    all_to_all x1, starting transfers between devices, local(): lax.all_to_all(modes, ('gx', 'gy'), split_axis=0, concat_axis=0, tiled=True)  15.2 us
    ppermute x3, starting transfers between devices, local(): lax.ppermute(source, 'col', [(i, (i + step) % 8) for i in range(8)])  13.6 us
    pallas_call x1, Pallas kernels, local(): pl.pallas_call(inverse_kernel, out_shape=jax.ShapeDtypeStruct((TX, YH, YL...  4.29 us
    ppermute x3, waiting for transfers between devices, local(): lax.ppermute(source, 'col', [(i, (i + step) % 8) for i in range(8)])  3.99 us
    pallas_call x1, Pallas kernels, local(): pl.pallas_call(forward_kernel, in_specs=[anywhere] * 4, out_shape=[pltpu....  3.86 us
    ppermute x1, starting transfers between devices, local(): partner = lax.ppermute(raw, 'col', [(i, i ^ 1) for i in range(8)])  1.92 us
  transfers between devices with their start and end apart: 5, of which 2 were waited for; matrix products, arithmetic and copies ran while one was open for 0% of the time, Pallas kernels for 2%

profile of v7, /device:TPU:8, one launch (start us, length us, event | category | flops | bytes accessed | tf_op | source)
XLA Modules:
  0.0 73.1 jit_solution(17562205761078880432)
XLA Ops:
  0.0 3.9 %forward.1 = (bf16[64,32,128]{2,1,0:T(8,128)(2,1)S(1)}, bf16[8,4,8,32,128]{4,3,2,1,0:T(8,128)(2,1)S(1)}) custom-call(bf16[8,4,8,32,128]{4,3,2,1,0:T(8,128)(2,1)} %bitcast.7, bf16[1024,256]{1,0:T(8,128)(2,1)} %constant.8.clone.depth_far.depth, bf16[1024,512]{1,0:T(8,128)(2,1)} %constant.9.clone.second_far.second, bf16[512,512]{1,0:T(8,128)(2,1)} %constant.10.clone.first_far), custom_call_target="tpu_custom_call" | custom-call | tf_op jit(solution)/shard_map/forward/pallas_call | solution.py:316
  3.9 0.0 copy-start.3
  3.9 0.8 %copy-done.3 = bf16[64,32,128]{2,1,0:T(8,128)(2,1)} copy-done((bf16[64,32,128]{2,1,0:T(8,128)(2,1)}, bf16[64,32,128]{2,1,0:T(8,128)(2,1)S(1)}, u32[]{:S(2)}) %copy-start.3) | copy-done | bytes 524312
  4.7 0.0 copy-start.8
  4.7 15.2 %all-to-all-start = ((bf16[64,32,128]{2,1,0:T(8,128)(2,1)}), bf16[64,32,128]{2,1,0:T(8,128)(2,1)}, u32[]{:S(2)}, u32[]{:S(2)}) async-start(bf16[64,32,128]{2,1,0:T(8,128)(2,1)} %copy-done.3), calls=%async_computation | async-start | bytes 1048576 | tf_op jit(solution)/shard_map/all_to_all | solution.py:332
  19.9 0.0 copy-done.4
  19.9 1.9 %collective-permute-start = (bf16[4,2,4,16,32]{4,3,2,1,0:T(8,128)(2,1)S(1)}, bf16[4,2,4,16,32]{4,3,2,1,0:T(8,128)(2,1)S(1)}, u32[]{:S(2)}, u32[]{:S(2)}) collective-permute-start(bf16[4,2,4,16,32]{4,3,2,1,0:T(8,128)(2,1)S(1)} %bitcast.5), channel_id=1, source_target_pairs={{0,1},{1,0},{2,3},{3,2},{4,5},{5,4},{6,7},{7,6},{8,9},{9,8},{10,11... | collective-permute-start | bytes 98312 | tf_op jit(solution)/shard_map/ppermute | solution.py:302
  21.9 1.3 %collective-permute-done.other = bf16[4,2,4,16,32]{4,3,2,1,0:T(8,128)(2,1)S(1)} collective-permute-done((bf16[4,2,4,16,32]{4,3,2,1,0:T(8,128)(2,1)S(1)}, bf16[4,2,4,16,32]{4,3,2,1,0:T(8,128)(2,1)S(1)}, u32[]{:S(2)}, u32[]{:S(2)}) %collective-permute-start) | collective-permute-done | bytes 32800 | tf_op jit(solution)/shard_map/ppermute | solution.py:302
  23.2 0.3 prepare.1.here
  23.5 6.8 %collective-permute-start.3 = (bf16[2,128,128]{2,1,0:T(8,128)(2,1)S(1)}, bf16[2,128,128]{2,1,0:T(8,128)(2,1)S(1)}, u32[]{:S(2)}, u32[]{:S(2)}) collective-permute-start(bf16[2,128,128]{2,1,0:T(8,128)(2,1)S(1)} %prepare.1.here), channel_id=1, source_target_pairs={{0,4},{1,5},{2,6},{3,7},{4,0},{5,1},{6,2},{7,3},{8,12},{9,13},{10,... | collective-permute-start | bytes 196616 | tf_op jit(solution)/shard_map/ppermute | solution.py:313
  30.3 3.1 %collective-permute-start.2 = (bf16[2,128,128]{2,1,0:T(8,128)(2,1)S(1)}, bf16[2,128,128]{2,1,0:T(8,128)(2,1)S(1)}, u32[]{:S(2)}, u32[]{:S(2)}) collective-permute-start(bf16[2,128,128]{2,1,0:T(8,128)(2,1)S(1)} %prepare.1.here), channel_id=1, source_target_pairs={{0,6},{1,7},{2,0},{3,1},{4,2},{5,3},{6,4},{7,5},{8,14},{9,15},{10,... | collective-permute-start | bytes 196616 | tf_op jit(solution)/shard_map/ppermute | solution.py:313
  33.5 3.6 %collective-permute-start.1 = (bf16[2,128,128]{2,1,0:T(8,128)(2,1)S(1)}, bf16[2,128,128]{2,1,0:T(8,128)(2,1)S(1)}, u32[]{:S(2)}, u32[]{:S(2)}) collective-permute-start(bf16[2,128,128]{2,1,0:T(8,128)(2,1)S(1)} %prepare.1.here), channel_id=1, source_target_pairs={{0,2},{1,3},{2,4},{3,5},{4,6},{5,7},{6,0},{7,1},{8,10},{9,11},{10,... | collective-permute-start | bytes 196616 | tf_op jit(solution)/shard_map/ppermute | solution.py:313
  37.1 0.0 all-to-all-done.parts_far
  37.1 0.0 copy-start.1
  37.1 0.0 copy-start.2
  37.1 1.3 %collect.1 = (f32[32,128]{1,0:T(8,128)S(1)}, f32[64,128]{1,0:T(8,128)S(1)}, f32[64,128]{1,0:T(8,128)S(1)}) custom-call(bf16[64,32,128]{2,1,0:T(8,128)(2,1)} %all-to-all-done.parts_far), custom_call_target="tpu_custom_call" | custom-call | tf_op jit(solution)/shard_map/collect/pallas_call | solution.py:335
  38.4 0.0 collective-permute-done.3.across
  38.4 0.0 collective-permute-done.2.after
  38.4 4.0 %collective-permute-done.1.before = bf16[2,128,128]{2,1,0:T(8,128)(2,1)S(1)} collective-permute-done((bf16[2,128,128]{2,1,0:T(8,128)(2,1)S(1)}, bf16[2,128,128]{2,1,0:T(8,128)(2,1)S(1)}, u32[]{:S(2)}, u32[]{:S(2)}) %collective-permute-start.1) | collective-permute-done | bytes 65568 | tf_op jit(solution)/shard_map/ppermute | solution.py:313
  42.4 0.5 mix.1
  42.9 25.8 %all_to_all.10.modes = bf16[64,32,128]{2,1,0:T(8,128)(2,1)S(1)} all-to-all(bf16[64,32,128]{2,1,0:T(8,128)(2,1)S(1)} %mix.1), channel_id=1, replica_groups=mesh['gx'=16,'gy'=4,'col'=8] {'gx','gy'}, dimensions={0} | all-to-all | bytes 1048576 | tf_op jit(solution)/shard_map/all_to_all | solution.py:353
  68.7 0.0 copy-done
  68.7 0.0 copy-done.5
  68.8 4.3 %inverse.1 = bf16[8,4,8,32,128]{4,3,2,1,0:T(8,128)(2,1)} custom-call(bf16[64,32,128]{2,1,0:T(8,128)(2,1)S(1)} %all_to_all.10.modes, bf16[8,4,8,32,128]{4,3,2,1,0:T(8,128)(2,1)S(1)} %get-tuple-element.14.fields, bf16[1024,256]{1,0:T(8,128)(2,1)S(1)} %copy-done.1, bf16[1024,512]{1,0:T(8,128)(2,1)S(1)} %copy-done, bf16[512,512]{1,0:T(8,128)(2,1)S(1)} %copy-done.2, ...), custom_call_target="tpu_custom_call" | custom-call | tf_op jit(solution)/shard_map/inverse/pallas_call | solution.py:354
  (10 shorter events, 0.0 us)
Async XLA Ops:
  0.0 19.9 %copy-start.4 = (bf16[1,1,4,2,32,4,16]{4,6,5,3,2,1,0:T(8,128)(2,1)S(1)}, bf16[1,1,4,2,32,4,16]{4,6,5,3,2,1,0:T(8,128)(2,1)}, u32[]{:S(2)}) copy-start(bf16[1,1,4,2,32,4,16]{4,6,5,3,2,1,0:T(8,128)(2,1)} %param.11) | copy-start | bytes 98308
  3.9 0.8 %copy-start.3 = (bf16[64,32,128]{2,1,0:T(8,128)(2,1)}, bf16[64,32,128]{2,1,0:T(8,128)(2,1)S(1)}, u32[]{:S(2)}) copy-start(bf16[64,32,128]{2,1,0:T(8,128)(2,1)S(1)} %get-tuple-element.10) | copy-start | bytes 1572868
  4.7 64.1 %copy-start = (bf16[1024,512]{1,0:T(8,128)(2,1)S(1)}, bf16[1024,512]{1,0:T(8,128)(2,1)}, u32[]{:S(2)}) copy-start(bf16[1024,512]{1,0:T(8,128)(2,1)} %constant.9.clone.second_far.second) | copy-start | bytes 3145732
  4.7 64.1 %copy-start.5 = (bf16[1,32,32]{2,1,0:T(8,128)(2,1)S(1)}, bf16[1,32,32]{2,1,0:T(8,128)(2,1)}, u32[]{:S(2)}) copy-start(bf16[1,32,32]{2,1,0:T(8,128)(2,1)} %skip.1) | copy-start | bytes 6148
  4.7 64.1 %copy-start.6 = (f32[1,32]{1,0:T(1,128)S(1)}, f32[1,32]{1,0:T(1,128)}, u32[]{:S(2)}) copy-start(f32[1,32]{1,0:T(1,128)} %bias_row.1) | copy-start | bytes 388
  4.7 64.1 %copy-start.7 = (f32[1,32]{1,0:T(1,128)S(1)}, f32[1,32]{1,0:T(1,128)}, u32[]{:S(2)}) copy-start(f32[1,32]{1,0:T(1,128)} %gain_row.1) | copy-start | bytes 388
  4.7 64.1 %copy-start.8 = (f32[1,32]{1,0:T(1,128)S(1)}, f32[1,32]{1,0:T(1,128)}, u32[]{:S(2)}) copy-start(f32[1,32]{1,0:T(1,128)} %shift_row.1) | copy-start | bytes 388
  4.7 32.4 %all-to-all-start = ((bf16[64,32,128]{2,1,0:T(8,128)(2,1)}), bf16[64,32,128]{2,1,0:T(8,128)(2,1)}, u32[]{:S(2)}, u32[]{:S(2)}) async-start(bf16[64,32,128]{2,1,0:T(8,128)(2,1)} %copy-done.3), calls=%async_computation | async-start | bytes 1048576 | tf_op jit(solution)/shard_map/all_to_all | solution.py:332
  19.9 3.2 %collective-permute-start = (bf16[4,2,4,16,32]{4,3,2,1,0:T(8,128)(2,1)S(1)}, bf16[4,2,4,16,32]{4,3,2,1,0:T(8,128)(2,1)S(1)}, u32[]{:S(2)}, u32[]{:S(2)}) collective-permute-start(bf16[4,2,4,16,32]{4,3,2,1,0:T(8,128)(2,1)S(1)} %bitcast.5), channel_id=1, source_target_pairs={{0,1},{1,0},{2,3},{3,2},{4,5},{5,4},{6,7},{7,6},{8,9},{9,8},{10,11... | collective-permute-start | bytes 98312 | tf_op jit(solution)/shard_map/ppermute | solution.py:302
  23.5 14.9 %collective-permute-start.3 = (bf16[2,128,128]{2,1,0:T(8,128)(2,1)S(1)}, bf16[2,128,128]{2,1,0:T(8,128)(2,1)S(1)}, u32[]{:S(2)}, u32[]{:S(2)}) collective-permute-start(bf16[2,128,128]{2,1,0:T(8,128)(2,1)S(1)} %prepare.1.here), channel_id=1, source_target_pairs={{0,4},{1,5},{2,6},{3,7},{4,0},{5,1},{6,2},{7,3},{8,12},{9,13},{10,... | collective-permute-start | bytes 196616 | tf_op jit(solution)/shard_map/ppermute | solution.py:313
  30.3 8.1 %collective-permute-start.2 = (bf16[2,128,128]{2,1,0:T(8,128)(2,1)S(1)}, bf16[2,128,128]{2,1,0:T(8,128)(2,1)S(1)}, u32[]{:S(2)}, u32[]{:S(2)}) collective-permute-start(bf16[2,128,128]{2,1,0:T(8,128)(2,1)S(1)} %prepare.1.here), channel_id=1, source_target_pairs={{0,6},{1,7},{2,0},{3,1},{4,2},{5,3},{6,4},{7,5},{8,14},{9,15},{10,... | collective-permute-start | bytes 196616 | tf_op jit(solution)/shard_map/ppermute | solution.py:313
  33.5 9.0 %collective-permute-start.1 = (bf16[2,128,128]{2,1,0:T(8,128)(2,1)S(1)}, bf16[2,128,128]{2,1,0:T(8,128)(2,1)S(1)}, u32[]{:S(2)}, u32[]{:S(2)}) collective-permute-start(bf16[2,128,128]{2,1,0:T(8,128)(2,1)S(1)} %prepare.1.here), channel_id=1, source_target_pairs={{0,2},{1,3},{2,4},{3,5},{4,6},{5,7},{6,0},{7,1},{8,10},{9,11},{10,... | collective-permute-start | bytes 196616 | tf_op jit(solution)/shard_map/ppermute | solution.py:313
  37.1 31.7 %copy-start.1 = (bf16[1024,256]{1,0:T(8,128)(2,1)S(1)}, bf16[1024,256]{1,0:T(8,128)(2,1)}, u32[]{:S(2)}) copy-start(bf16[1024,256]{1,0:T(8,128)(2,1)} %constant.8.clone.depth_far.depth) | copy-start | bytes 1572868
  37.1 31.7 %copy-start.2 = (bf16[512,512]{1,0:T(8,128)(2,1)S(1)}, bf16[512,512]{1,0:T(8,128)(2,1)}, u32[]{:S(2)}) copy-start(bf16[512,512]{1,0:T(8,128)(2,1)} %constant.11.clone.first) | copy-start | bytes 1572868
